TPU v7x, 64 devices: a 2x2x8 block of a 4x4x8 slice. The times are simulated.
64 devices in a mesh: data: 4 (over x, y), dap: 16 (over z, core).
Axes of the slice: x: 2, y: 2, z: 8, core: 2. Of those that a mesh axis runs over, the one named last changes fastest.
The devices are a block of a 4x4x8 slice.
Arguments:
- pair_act: bfloat16 [2048, 512, 128], P(('data', 'dap')), parts along dimension 0
- pair_mask: int32 [2048, 512], P(('data', 'dap')), parts along dimension 0
- d_pair_out: bfloat16 [2048, 512, 128], P(('data', 'dap')), parts along dimension 0
- ln_pair: bfloat16 [2, 2, 128], replicated
- w_proj: bfloat16 [2, 128, 512], replicated
- w_gate: bfloat16 [2, 128, 128], replicated
- ln_chan: bfloat16 [2, 2, 128], replicated
- w_out: bfloat16 [2, 128, 128], replicated
Outputs:
- output 1: bfloat16 [2048, 512, 128], P(('data', 'dap')), parts along dimension 0
- output 2: bfloat16 [2048, 512, 128], P(('data', 'dap')), parts along dimension 0
- output 3: bfloat16 [8, 2, 128], P('data'), parts along dimension 0
- output 4: bfloat16 [8, 128, 512], P('data'), parts along dimension 0
- output 5: bfloat16 [8, 128, 128], P('data'), parts along dimension 0
- output 6: bfloat16 [8, 2, 128], P('data'), parts along dimension 0
- output 7: bfloat16 [8, 128, 128], P('data'), parts along dimension 0
There are 4 independent parts. A program takes and returns all parts, laid end to end along the dimension named above; an argument that names none is the same for every part.
All inputs are finite; a program needn't handle non-finite values.
Results may differ from a plain program's by a relative error of at most 0.02.
Values are sent between devices in bfloat16 or wider.
A program may use at most 768 MiB of HBM per device.

v0:
```python
import jax
import jax.numpy as jnp
from jax import lax
from jax.sharding import PartitionSpec as P

LN_EPS = 1e-5
GROUP_AXIS = 'dap'


def layer_norm(values, gain_vec, shift_vec, norm_axis):
    mean_val = jnp.mean(values, axis=norm_axis, keepdims=True)
    centered = values - mean_val
    variance = jnp.mean(centered * centered, axis=norm_axis, keepdims=True)
    return centered * lax.rsqrt(variance + LN_EPS) * gain_vec + shift_vec


def norm_pair(values, ln_params):
    return layer_norm(values, ln_params[0], ln_params[1], -1)


def norm_chan(values, ln_params):
    return layer_norm(values, ln_params[0][:, None, None], ln_params[1][:, None, None], 0)


def to_channels(row_blocks):
    chan_dim = row_blocks.ndim - 3
    return lax.all_to_all(row_blocks, GROUP_AXIS, chan_dim, chan_dim + 1, tiled=True)


def to_rows(chan_blocks):
    chan_dim = chan_blocks.ndim - 3
    return lax.all_to_all(chan_blocks, GROUP_AXIS, chan_dim + 1, chan_dim, tiled=True)


def update_forward(z_rows, mask_f, ln_p, w_proj, w_gate, ln_q, w_out, incoming):
    z_float = z_rows.astype(jnp.float32)
    x_float, pair_back = jax.vjp(norm_pair, z_float, ln_p.astype(jnp.float32))
    x_norm = x_float.astype(jnp.bfloat16)
    proj_all = jnp.einsum('ijd,de->eij', x_norm, w_proj, preferred_element_type=jnp.float32)
    gate_val = jax.nn.sigmoid(jnp.einsum('ijd,de->ije', x_norm, w_gate, preferred_element_type=jnp.float32))
    lin_a, pre_ga, lin_b, pre_gb = jnp.split(proj_all, 4, axis=0)
    sig_a = jax.nn.sigmoid(pre_ga)
    sig_b = jax.nn.sigmoid(pre_gb)
    left_proj = (mask_f * sig_a * lin_a).astype(jnp.bfloat16)
    right_proj = (mask_f * sig_b * lin_b).astype(jnp.bfloat16)
    chan_pair = to_channels(jnp.stack([left_proj, right_proj]))
    if incoming:
        tri_prod = jnp.einsum('cki,ckj->cij', chan_pair[0], chan_pair[1], preferred_element_type=jnp.float32)
    else:
        tri_prod = jnp.einsum('cik,cjk->cij', chan_pair[0], chan_pair[1], preferred_element_type=jnp.float32)
    t_rows = to_rows(tri_prod.astype(jnp.bfloat16))
    y_float, chan_back = jax.vjp(norm_chan, t_rows.astype(jnp.float32), ln_q.astype(jnp.float32))
    y_norm = y_float.astype(jnp.bfloat16)
    update_f = jnp.einsum('cij,cd->ijd', y_norm, w_out, preferred_element_type=jnp.float32)
    z_new = (z_float + gate_val * update_f).astype(jnp.bfloat16)
    saved_fwd = dict(pair_back=pair_back, chan_back=chan_back, x_norm=x_norm, lin_a=lin_a, sig_a=sig_a, lin_b=lin_b, sig_b=sig_b, chan_pair=chan_pair, y_norm=y_norm, update_f=update_f, gate_val=gate_val)
    return z_new, saved_fwd


def update_backward(d_new, saved_fwd, mask_f, w_proj, w_gate, w_out, incoming):
    d_newf = d_new.astype(jnp.float32)
    gate_val = saved_fwd['gate_val']
    d_gate = (d_newf * saved_fwd['update_f'] * gate_val * (1.0 - gate_val)).astype(jnp.bfloat16)
    d_update = (d_newf * gate_val).astype(jnp.bfloat16)
    g_w_out = jnp.einsum('cij,ijd->cd', saved_fwd['y_norm'], d_update, preferred_element_type=jnp.float32)
    d_y = jnp.einsum('ijd,cd->cij', d_update, w_out, preferred_element_type=jnp.float32).astype(jnp.bfloat16)
    d_t, g_ln_q = saved_fwd['chan_back'](d_y.astype(jnp.float32))
    d_chan = to_channels(d_t.astype(jnp.bfloat16))
    left_chan = saved_fwd['chan_pair'][0]
    right_chan = saved_fwd['chan_pair'][1]
    if incoming:
        d_left = jnp.einsum('ckj,cij->cki', right_chan, d_chan, preferred_element_type=jnp.float32)
        d_right = jnp.einsum('cki,cij->ckj', left_chan, d_chan, preferred_element_type=jnp.float32)
    else:
        d_left = jnp.einsum('cij,cjk->cik', d_chan, right_chan, preferred_element_type=jnp.float32)
        d_right = jnp.einsum('cij,cik->cjk', d_chan, left_chan, preferred_element_type=jnp.float32)
    d_rows = to_rows(jnp.stack([d_left.astype(jnp.bfloat16), d_right.astype(jnp.bfloat16)]))
    d_left_f = d_rows[0].astype(jnp.float32) * mask_f
    d_right_f = d_rows[1].astype(jnp.float32) * mask_f
    sig_a = saved_fwd['sig_a']
    sig_b = saved_fwd['sig_b']
    d_proj = jnp.concatenate([d_left_f * sig_a, d_left_f * saved_fwd['lin_a'] * sig_a * (1.0 - sig_a), d_right_f * sig_b, d_right_f * saved_fwd['lin_b'] * sig_b * (1.0 - sig_b)], axis=0).astype(jnp.bfloat16)
    x_norm = saved_fwd['x_norm']
    g_w_proj = jnp.einsum('ijd,eij->de', x_norm, d_proj, preferred_element_type=jnp.float32)
    g_w_gate = jnp.einsum('ijd,ije->de', x_norm, d_gate, preferred_element_type=jnp.float32)
    d_x = (jnp.einsum('eij,de->ijd', d_proj, w_proj, preferred_element_type=jnp.float32) + jnp.einsum('ije,de->ijd', d_gate, w_gate, preferred_element_type=jnp.float32)).astype(jnp.bfloat16)
    d_zf, g_ln_p = saved_fwd['pair_back'](d_x.astype(jnp.float32))
    d_prev = (d_newf + d_zf).astype(jnp.bfloat16)
    return d_prev, (g_ln_p, g_w_proj, g_w_gate, g_ln_q, g_w_out)


def solution(mesh):
    row_spec = P(('data', 'dap'), None, None)
    mask_spec = P(('data', 'dap'), None)
    full_spec = P()
    grad_spec = P('data', None, None)

    def device_step(pair_act, pair_mask, d_pair_out, ln_pair, w_proj, w_gate, ln_chan, w_out):
        mask_f = pair_mask.astype(jnp.float32)
        z_mid, saved_out = update_forward(pair_act, mask_f, ln_pair[0], w_proj[0], w_gate[0], ln_chan[0], w_out[0], False)
        pair_out, saved_in = update_forward(z_mid, mask_f, ln_pair[1], w_proj[1], w_gate[1], ln_chan[1], w_out[1], True)
        d_mid, grads_in = update_backward(d_pair_out, saved_in, mask_f, w_proj[1], w_gate[1], w_out[1], True)
        d_pair, grads_out = update_backward(d_mid, saved_out, mask_f, w_proj[0], w_gate[0], w_out[0], False)
        local_grads = tuple(jnp.stack([grad_a, grad_b]) for grad_a, grad_b in zip(grads_out, grads_in))
        group_grads = lax.psum(local_grads, GROUP_AXIS)
        return (pair_out, d_pair) + tuple(grad_sum.astype(jnp.bfloat16) for grad_sum in group_grads)

    return jax.shard_map(device_step, mesh=mesh, in_specs=(row_spec, mask_spec, row_spec, full_spec, full_spec, full_spec, full_spec, full_spec), out_specs=(row_spec, row_spec, grad_spec, grad_spec, grad_spec, grad_spec, grad_spec), check_vma=False)
```

profile of v0, /device:TPU:23, one launch (start us, length us, event | category | flops | bytes accessed | tf_op | source)
XLA Modules:
  0.0 1712.8 jit_solution(2802821040900619463)
XLA Ops:
  15.4 13.4 convolution_bitcast_fusion.1
  28.9 15.6 fusion.86
  50.6 11.4 copy.244
  62.0 195.1 %all_to_all.114 = bf16[2,128,32,512]{3,2,0,1:T(8,128)(2,1)} all-to-all(bf16[2,128,32,512]{3,2,0,1:T(8,128)(2,1)} %copy.244), channel_id=1, replica_groups=mesh['data'=4,'dap'=16] {'dap'}, dimensions={1} | all-to-all | bytes 16777216 | tf_op jit(solution)/shard_map/all_to_all | solution.py:27
  284.5 91.5 %all-to-all-done.1 = bf16[8,512,512]{2,0,1:T(8,128)(2,1)} async-done(((bf16[8,512,512]{2,0,1:T(8,128)(2,1)}), bf16[8,512,512]{2,0,1:T(8,128)(2,1)}, u32[]{:S(2)}, u32[]{:S(2)}) %all-to-all-start.1) | async-done | bytes 4194336 | tf_op jit(solution)/shard_map/all_to_all | solution.py:32
  409.6 13.2 convolution_bitcast_fusion
  422.8 15.6 fusion.88
  444.8 11.4 copy.257
  456.2 192.8 %all_to_all.115 = bf16[2,128,32,512]{3,2,0,1:T(8,128)(2,1)} all-to-all(bf16[2,128,32,512]{3,2,0,1:T(8,128)(2,1)} %copy.257), channel_id=1, replica_groups=mesh['data'=4,'dap'=16] {'dap'}, dimensions={1} | all-to-all | bytes 16777216 | tf_op jit(solution)/shard_map/all_to_all | solution.py:27
  691.6 77.9 %all-to-all-done.3 = bf16[8,512,512]{2,0,1:T(8,128)(2,1)} async-done(((bf16[8,512,512]{2,0,1:T(8,128)(2,1)}), bf16[8,512,512]{2,0,1:T(8,128)(2,1)}, u32[]{:S(2)}, u32[]{:S(2)}) %all-to-all-start.3) | async-done | bytes 4194336 | tf_op jit(solution)/shard_map/all_to_all | solution.py:32
  805.5 10.8 fusion.26
  816.3 10.9 add_convert_fusion.5
  835.1 103.2 %all_to_all.116 = bf16[128,32,512]{2,1,0:T(8,128)(2,1)S(1)} all-to-all(bf16[128,32,512]{2,1,0:T(8,128)(2,1)} %copy.273), channel_id=1, replica_groups=mesh['data'=4,'dap'=16] {'dap'}, dimensions={0} | all-to-all | bytes 8388608 | tf_op jit(solution)/shard_map/all_to_all | solution.py:27
  951.5 11.4 copy.275
  1002.4 154.0 %all-to-all-done.5 = bf16[2,8,512,512]{3,1,0,2:T(8,128)(2,1)} async-done(((bf16[2,8,512,512]{3,1,0,2:T(8,128)(2,1)}), bf16[2,8,512,512]{3,1,0,2:T(8,128)(2,1)}, u32[]{:S(2)}, u32[]{:S(2)}) %all-to-all-start.5) | async-done | bytes 8388640 | tf_op jit(solution)/shard_map/all_to_all | solution.py:32
  1164.3 21.1 %fusion.78 = (bf16[128,32,512]{2,0,1:T(8,128)(2,1)}, bf16[128,32,512]{2,0,1:T(8,128)(2,1)}, bf16[128,32,512]{2,0,1:T(8,128)(2,1)}, bf16[128,32,512]{2,0,1:T(8,128)(2,1)}) fusion(f32[32,512]{1,0:T(8,128)S(1)} %convert_element_type.227, bf16[2,16,8,32,512]{4,2,1,3,0:T(8,128)(2,1)} %bitcast.293, f32[512,32,512]{2,0,1:T(8,128)} %convolution_bitcast_fusion), kind=kLoop, calls=%fused_computation.120 | loop fusion | flops 50331648 | bytes 58785792 | tf_op jit(solution)/shard_map/convert.18
  1211.7 13.0 fusion.43
  1233.2 10.8 fusion.27
  1244.1 10.9 add_convert_fusion.3
  1262.9 103.2 %all_to_all.117 = bf16[128,32,512]{2,1,0:T(8,128)(2,1)S(1)} all-to-all(bf16[128,32,512]{2,1,0:T(8,128)(2,1)} %copy.287), channel_id=1, replica_groups=mesh['data'=4,'dap'=16] {'dap'}, dimensions={0} | all-to-all | bytes 8388608 | tf_op jit(solution)/shard_map/all_to_all | solution.py:27
  1379.4 11.4 copy.290
  1445.2 138.9 %all-to-all-done.7 = bf16[2,8,512,512]{3,1,0,2:T(8,128)(2,1)} async-done(((bf16[2,8,512,512]{3,1,0,2:T(8,128)(2,1)}), bf16[2,8,512,512]{3,1,0,2:T(8,128)(2,1)}, u32[]{:S(2)}, u32[]{:S(2)}) %all-to-all-start.7) | async-done | bytes 8388640 | tf_op jit(solution)/shard_map/all_to_all | solution.py:32
  1592.0 20.0 %fusion.66 = (bf16[128,32,512]{2,0,1:T(8,128)(2,1)S(1)}, bf16[128,32,512]{2,0,1:T(8,128)(2,1)}, bf16[128,32,512]{2,0,1:T(8,128)(2,1)}, bf16[128,32,512]{2,0,1:T(8,128)(2,1)}) fusion(f32[32,512]{1,0:T(8,128)S(1)} %copy-done.42, bf16[2,16,8,32,512]{4,2,1,3,0:T(8,128)(2,1)} %bitcast.292, f32[512,32,512]{2,0,1:T(8,128)} %convolution_bitcast_fusion.1), kind=kLoop, calls=%fused_computation.106 | loop fusion | flops 50331648 | bytes 58785792 | tf_op jit(solution)/shard_map/convert.14
  1660.4 52.0 %all-reduce.10 = (bf16[2,2,128]{2,1,0:T(2,128)(2,1)}, bf16[2,128,512]{2,1,0:T(8,128)(2,1)}, bf16[2,128,128]{2,1,0:T(8,128)(2,1)}, bf16[2,2,128]{2,1,0:T(2,128)(2,1)}, bf16[2,128,128]{2,1,0:T(8,128)(2,1)}) all-reduce(f32[2,2,128]{2,1,0:T(2,128)S(1)} %pad_maximum_fusion.17, ...), channel_id=1, replica_groups=mesh['data'=4,'dap'=16] {'dap'}, use_global_device_ids=true, to_apply=%region_20.0 | all-reduce | flops 197632 | bytes 1185792 | tf_op jit(solution)/shard_map/psum | solution.py:105
  (277 shorter events, 401.0 us)
Async XLA Ops:
  2.2 1162.2 %copy-start.41 = (f32[32,512]{1,0:T(8,128)}, f32[32,512]{1,0:T(8,128)S(1)}, u32[]{:S(2)}) copy-start(f32[32,512]{1,0:T(8,128)S(1)} %convert_element_type.227) | copy-start | bytes 196612
  2.2 13.3 copy-start.53
  11.8 384.5 %copy-start.31 = (f32[32,512]{1,0:T(8,128)}, f32[32,512]{1,0:T(8,128)S(1)}, u32[]{:S(2)}) copy-start(f32[32,512]{1,0:T(8,128)S(1)} %broadcast_multiply_fusion.3) | copy-start | bytes 196612
  15.3 13.5 copy-start.45
  15.4 380.9 %copy-start.37 = (f32[32,512]{1,0:T(8,128)}, f32[32,512]{1,0:T(8,128)S(1)}, u32[]{:S(2)}) copy-start(f32[32,512]{1,0:T(8,128)S(1)} %fusion.122) | copy-start | bytes 196612
  15.4 380.9 %copy-start.61 = (f32[128]{0:T(128)}, f32[128]{0:T(128)S(1)}, u32[]{:S(2)}) copy-start(f32[128]{0:T(128)S(1)} %get-tuple-element.115) | copy-start | bytes 1540
  15.4 380.9 %copy-start.68 = (f32[128]{0:T(128)}, f32[128]{0:T(128)S(1)}, u32[]{:S(2)}) copy-start(f32[128]{0:T(128)S(1)} %get-tuple-element.114) | copy-start | bytes 1540
  15.4 390.1 %copy-start.66 = (f32[128]{0:T(128)}, f32[128]{0:T(128)S(1)}, u32[]{:S(2)}) copy-start(f32[128]{0:T(128)S(1)} %get-tuple-element.101) | copy-start | bytes 1540
  278.0 98.0 %all-to-all-start.1 = ((bf16[8,512,512]{2,0,1:T(8,128)(2,1)}), bf16[8,512,512]{2,0,1:T(8,128)(2,1)}, u32[]{:S(2)}, u32[]{:S(2)}) async-start(bf16[8,512,512]{2,0,1:T(8,128)(2,1)} %copy.246), calls=%async_computation.1 | async-start | bytes 8388608 | tf_op jit(solution)/shard_map/all_to_all | solution.py:32
  284.2 532.1 %copy-start.64 = (f32[128]{0:T(128)}, f32[128]{0:T(128)S(1)}, u32[]{:S(2)}) copy-start(f32[128]{0:T(128)S(1)} %get-tuple-element.96) | copy-start | bytes 1540
  671.7 97.8 %all-to-all-start.3 = ((bf16[8,512,512]{2,0,1:T(8,128)(2,1)}), bf16[8,512,512]{2,0,1:T(8,128)(2,1)}, u32[]{:S(2)}, u32[]{:S(2)}) async-start(bf16[8,512,512]{2,0,1:T(8,128)(2,1)} %copy.262), calls=%async_computation.3 | async-start | bytes 8388608 | tf_op jit(solution)/shard_map/all_to_all | solution.py:32
  835.1 103.5 %copy-start.28 = (bf16[1,8,16,32,512]{4,3,2,1,0:T(8,128)(2,1)S(1)}, bf16[1,8,16,32,512]{4,3,2,1,0:T(8,128)(2,1)}, u32[]{:S(2)}) copy-start(bf16[1,8,16,32,512]{4,3,2,1,0:T(8,128)(2,1)} %copy-done.27) | copy-start | bytes 12582916
  963.0 193.4 %all-to-all-start.5 = ((bf16[2,8,512,512]{3,1,0,2:T(8,128)(2,1)}), bf16[2,8,512,512]{3,1,0,2:T(8,128)(2,1)}, u32[]{:S(2)}, u32[]{:S(2)}) async-start(bf16[2,8,512,512]{3,1,0,2:T(8,128)(2,1)} %copy.275), calls=%async_computation.5 | async-start | bytes 16777216 | tf_op jit(solution)/shard_map/all_to_all | solution.py:32
  1164.3 21.1 %copy-start.54 = (bf16[2,128,512]{2,1,0:T(8,128)(2,1)S(1)}, bf16[2,128,512]{2,1,0:T(8,128)(2,1)}, u32[]{:S(2)}) copy-start(bf16[2,128,512]{2,1,0:T(8,128)(2,1)} %param.12) | copy-start | bytes 786436
  1195.7 10.9 copy-start.8
  1206.6 18.0 %slice-start = ((s8[8388608]{0:T(1024)(128)(4,1)}), s8[4194304]{0:T(1024)(128)(4,1)S(1)}, s32[]{:S(2)}) async-start(s8[8388608]{0:T(1024)(128)(4,1)} %bitcast.277), calls=%async_computation.8 | async-start | bytes 8388608
  1211.6 13.0 slice-start.1
  1211.7 13.0 copy-start.34
  1211.7 13.0 copy-start.63
  1262.9 103.6 %copy-start.21 = (bf16[1,8,16,32,512]{4,3,2,1,0:T(8,128)(2,1)S(1)}, bf16[1,8,16,32,512]{4,3,2,1,0:T(8,128)(2,1)}, u32[]{:S(2)}) copy-start(bf16[1,8,16,32,512]{4,3,2,1,0:T(8,128)(2,1)} %copy-done.20) | copy-start | bytes 12582916
  1390.8 193.3 %all-to-all-start.7 = ((bf16[2,8,512,512]{3,1,0,2:T(8,128)(2,1)}), bf16[2,8,512,512]{3,1,0,2:T(8,128)(2,1)}, u32[]{:S(2)}, u32[]{:S(2)}) async-start(bf16[2,8,512,512]{3,1,0,2:T(8,128)(2,1)} %copy.290), calls=%async_computation.7 | async-start | bytes 16777216 | tf_op jit(solution)/shard_map/all_to_all | solution.py:32
  1406.8 16.3 slice-start.2
  1406.8 16.3 slice-start.4
  1592.0 22.0 %copy-start.3 = (bf16[32,512,128]{1,2,0:T(8,128)(2,1)S(1)}, bf16[32,512,128]{1,2,0:T(8,128)(2,1)}, u32[]{:S(2)}) copy-start(bf16[32,512,128]{1,2,0:T(8,128)(2,1)} %copy.239) | copy-start | bytes 12582916
  (63 other events, 412.4 us)
where the time goes:
time: 1720 us; the launch traced here: 1710 us
  blocking collectives  646 us (38%)
  waiting for transfers between devices  462 us (27%)
  other arithmetic  221 us (13%)
  local copies, waits for them, and re-layouts  186 us (11%)
  matrix products  175 us (10%)
  starting transfers between devices  20.4 us (1%)
    all_to_all x4, blocking collectives, to_channels(): lax.all_to_all(row_blocks, GROUP_AXIS, chan_dim, chan_dim + 1, tiled=True)  594 us
    all_to_all x4, waiting for transfers between devices, to_rows(): lax.all_to_all(chan_blocks, GROUP_AXIS, chan_dim + 1, chan_dim, tiled=True)  462 us
    psum x1, blocking collectives, device_step(): group_grads = lax.psum(local_grads, GROUP_AXIS)  52 us
    another operation x4, other arithmetic, update_forward(): chan_pair = to_channels(jnp.stack([left_proj, right_proj]))  43.7 us
    another operation x2, other arithmetic  41.1 us
    reduce_sum x6, other arithmetic, layer_norm(): return centered * lax.rsqrt(variance + LN_EPS) * gain_vec + shift_vec  38.5 us
    unnamed x170, local copies, waits for them, and re-layouts  38.3 us
  transfers between devices with their start and end apart: 4, of which 4 were waited for; matrix products, arithmetic and copies ran while one was open for 6% of the time, Pallas kernels for 0%

commit v1 on v0

v1 whole, which is shorter than its diff:
```python
import functools

import jax
import jax.numpy as jnp
from jax import lax
from jax.experimental import pallas as pl
from jax.experimental.pallas import tpu as pltpu
from jax.sharding import PartitionSpec as P

LN_EPS = 1e-5
AXIS = 'dap'
F32 = jnp.float32
BF16 = jnp.bfloat16
RB = 16
KB = 256
MESH_ID = pl.DeviceIdType.MESH
ANY = pl.BlockSpec(memory_space=pl.ANY)
VM = pl.BlockSpec(memory_space=pltpu.VMEM)


def dot(lhs, rhs, lc, rc):
    return lax.dot_general(lhs, rhs, (((lc,), (rc,)), ((), ())), preferred_element_type=F32)


def norm(values, axis):
    mean = jnp.mean(values, axis=axis, keepdims=True)
    cent = values - mean
    var = jnp.mean(cent * cent, axis=axis, keepdims=True)
    rstd = lax.rsqrt(var + LN_EPS)
    return cent * rstd, rstd


def enter(n):
    me = lax.axis_index(AXIS)
    bar = pltpu.get_barrier_semaphore()

    def greet(s, carry):
        pl.semaphore_signal(bar, inc=1, device_id={AXIS: lax.rem(me + s, n)}, device_id_type=MESH_ID)
        return carry

    lax.fori_loop(1, n, greet, 0)
    pl.semaphore_wait(bar, n - 1)
    return me


def scatter(n, me, src, dst, ssem, rsem):
    def one(s, carry):
        peer = lax.rem(me + s, n)
        pltpu.make_async_remote_copy(src_ref=src(peer), dst_ref=dst(me), send_sem=ssem, recv_sem=rsem, device_id={AXIS: peer}, device_id_type=MESH_ID).start()
        return carry

    lax.fori_loop(1, n, one, 0)


def drain(ref, sem):
    pltpu.make_async_copy(ref, ref, sem).wait()


def block(q, n_cols):
    per = n_cols // KB
    i0 = pl.multiple_of((q // per) * RB, RB)
    k0 = pl.multiple_of(lax.rem(q, per) * KB, KB)
    return pl.ds(i0, RB), pl.ds(k0, KB), i0


def pack(s_ref, e0, count, write):
    def one(e, carry):
        off = pl.multiple_of(e * 8, 8)
        val = s_ref[:, pl.ds(e0 + off, 8), :]
        write(pl.ds(off, 8), jnp.swapaxes(val, 0, 1).astype(BF16))
        return carry

    lax.fori_loop(0, count // 8, one, 0)


def unpack(read, count, write):
    def one(e, carry):
        sl = pl.ds(pl.multiple_of(e * 16, 16), 16)
        write(sl, jnp.swapaxes(read(sl).astype(F32), 0, 1).astype(BF16))
        return carry

    lax.fori_loop(0, count // 16, one, 0)


def project(s_ref, i, x_row, m_row, wpt_ref, c):
    p = dot(wpt_ref[...], x_row, 1, 1)
    s_ref[i, 0:c, :] = m_row * jax.nn.sigmoid(p[c:2 * c]) * p[0:c]
    s_ref[i, c:2 * c, :] = m_row * jax.nn.sigmoid(p[3 * c:]) * p[2 * c:3 * c]


def fold_rows(v):
    return jnp.sum(v.reshape(v.shape[0] // 8, 8, v.shape[1]), axis=0)


def fold_lanes(v):
    out = v[:, 0:128]
    for h in range(1, v.shape[1] // 128):
        out = out + v[:, h * 128:(h + 1) * 128]
    return out


def send_ab(n, me, q, ri, rk, ab_send, ab_chan, rows, cl, sems):
    ssem, rsem, lsem = sems
    mine = pl.ds(me * rows, rows)
    row0 = me * rows

    def src(peer):
        return ab_send.at[:, pl.ds(peer * cl, cl), ri, rk]

    def dst(dev):
        return ab_chan.at[:, :, pl.ds(pl.multiple_of(dev * rows + ri.start, RB), RB), rk]

    pltpu.make_async_copy(src(me), dst(me), lsem).start()
    scatter(n, me, src, dst, ssem.at[q], rsem.at[q])


def finish_ab(n, nq, ab_send, ab_chan, rows, cl, sems):
    ssem, rsem, lsem = sems
    whole = ab_chan.at[:, :, pl.ds(0, rows), :]
    drain(whole, lsem)
    part = ab_chan.at[:, :, pl.ds(0, RB * (n - 1)), pl.ds(0, KB)]

    def one(q, carry):
        drain(part, ssem.at[q])
        drain(part, rsem.at[q])
        return carry

    lax.fori_loop(0, nq, one, 0)


def first_kernel(n, z_hbm, m_ref, gp_ref, wpt_ref, x_out, ab_chan, z_v, x_v, ab_send, s_ref, isem, osem, ssem, rsem, lsem):
    rows, cols, c = z_v.shape
    cl = c // n
    nq = (rows // RB) * (cols // KB)
    load = pltpu.make_async_copy(z_hbm, z_v, isem)
    load.start()
    me = enter(n)
    load.wait()
    sems = (ssem, rsem, lsem)

    def step(q, carry):
        ri, rk, i0 = block(q, cols)

        def row(i, carry2):
            xh, _ = norm(z_v[i0 + i, rk, :].astype(F32), -1)
            x_row = (xh * gp_ref[0:1, :] + gp_ref[1:2, :]).astype(BF16)
            x_v[i0 + i, rk, :] = x_row
            project(s_ref, i, x_row, m_ref[pl.ds(i0 + i, 1), rk], wpt_ref, c)
            return carry2

        lax.fori_loop(0, RB, row, 0)
        for h in range(2):
            def write(sl, val, h=h):
                ab_send[h, sl, ri, rk] = val
            pack(s_ref, h * c, c, write)
        send_ab(n, me, q, ri, rk, ab_send, ab_chan, rows, cl, sems)
        pltpu.make_async_copy(x_v.at[ri, rk, :], x_out.at[ri, rk, :], osem).start()
        return carry

    lax.fori_loop(0, nq, step, 0)
    drain(x_v, osem)
    finish_ab(n, nq, ab_send, ab_chan, rows, cl, sems)


def send_t(n, me, nq, cols, t_send, t_recv, rows, cl, ssem, rsem):
    def one(q, carry):
        ri, rk, i0 = block(q, cols)

        def src(peer):
            return t_send.at[:, pl.ds(pl.multiple_of(peer * rows + i0, RB), RB), rk]

        def dst(dev):
            return t_recv.at[pl.ds(dev * cl, cl), ri, rk]

        scatter(n, me, src, dst, ssem.at[q], rsem.at[q])
        return carry

    lax.fori_loop(0, nq, one, 0)

    def own(k, carry):
        t_recv[me * cl + k, :, :] = t_send[k, pl.ds(pl.multiple_of(me * rows, RB), rows), :]
        return carry

    lax.fori_loop(0, cl, own, 0)


def mid_kernel(n, ab_hbm, z_hbm, x_hbm, m_ref, gq_ref, wo_ref, wg_ref, gp_ref, wpt_ref,
               z_out, x_out, t_out, ab_chan,
               ab_v, z_v, x_v, t_send, t_recv, t_v, ab_send, s_ref, isem, osem, tss, trs, ssem, rsem, lsem):
    rows, cols, c = z_v.shape
    cl = c // n
    nq = (rows // RB) * (cols // KB)
    loads = [pltpu.make_async_copy(a, b, isem.at[k]) for k, (a, b) in enumerate(((ab_hbm, ab_v), (z_hbm, z_v), (x_hbm, x_v)))]
    for ld in loads:
        ld.start()
    me = enter(n)
    loads[0].wait()

    def tri(k, carry):
        t_send[k, :, :] = dot(ab_v[0, k], ab_v[1, k], 1, 1).astype(BF16)
        return carry

    lax.fori_loop(0, cl, tri, 0)
    send_t(n, me, nq, cols, t_send, t_recv, rows, cl, tss, trs)
    loads[1].wait()
    loads[2].wait()
    sems = (ssem, rsem, lsem)

    def step(q, carry):
        ri, rk, i0 = block(q, cols)
        drain(t_recv.at[pl.ds(0, c - cl), ri, rk], trs.at[q])

        def write_t(sl, val):
            t_v[ri, sl, rk] = val

        unpack(lambda sl: t_recv[sl, ri, rk], c, write_t)

        def row(i, carry2):
            r = i0 + i
            th, _ = norm(t_v[r, :, rk].astype(F32), 0)
            y = (th * gq_ref[0] + gq_ref[1]).astype(BF16)
            upd = dot(y, wo_ref[...], 0, 0)
            gate = jax.nn.sigmoid(dot(x_v[r, rk, :], wg_ref[...], 1, 0))
            z_new = (z_v[r, rk, :].astype(F32) + gate * upd).astype(BF16)
            z_v[r, rk, :] = z_new
            xh, _ = norm(z_new.astype(F32), -1)
            x_row = (xh * gp_ref[0:1, :] + gp_ref[1:2, :]).astype(BF16)
            x_v[r, rk, :] = x_row
            project(s_ref, i, x_row, m_ref[pl.ds(r, 1), rk], wpt_ref, c)
            return carry2

        lax.fori_loop(0, RB, row, 0)
        for h in range(2):
            def write(sl, val, h=h):
                ab_send[h, sl, ri, rk] = val
            pack(s_ref, h * c, c, write)
        send_ab(n, me, q, ri, rk, ab_send, ab_chan, rows, cl, sems)
        pltpu.make_async_copy(z_v.at[ri, rk, :], z_out.at[ri, rk, :], osem.at[0]).start()
        pltpu.make_async_copy(x_v.at[ri, rk, :], x_out.at[ri, rk, :], osem.at[1]).start()
        pltpu.make_async_copy(t_v.at[ri, :, rk], t_out.at[ri, :, rk], osem.at[2]).start()
        return carry

    lax.fori_loop(0, nq, step, 0)
    drain(z_v, osem.at[0])
    drain(x_v, osem.at[1])
    drain(t_v, osem.at[2])

    def sent(q, carry):
        drain(t_recv.at[pl.ds(0, c - cl), pl.ds(0, RB), pl.ds(0, KB)], tss.at[q])
        return carry

    lax.fori_loop(0, nq, sent, 0)
    finish_ab(n, nq, ab_send, ab_chan, rows, cl, sems)


def finish_back(i, r, rk, dn, th, rstd, y, upd, gate, gq_ref, wo_ref, dg_v, s_ref, gwo_ref, glq_ref):
    d_gate = dn * upd * gate * (1.0 - gate)
    d_upd = (dn * gate).astype(BF16)
    dg_v[r, rk, :] = d_gate.astype(BF16)
    gwo_ref[...] += dot(y, d_upd, 1, 0)
    dy = dot(wo_ref[...], d_upd, 1, 1).astype(BF16).astype(F32)
    glq_ref[0] += fold_lanes(dy * th)
    glq_ref[1] += fold_lanes(dy)
    dyg = dy * gq_ref[0]
    m1 = jnp.mean(dyg, axis=0, keepdims=True)
    m2 = jnp.mean(dyg * th, axis=0, keepdims=True)
    s_ref[i] = rstd * (dyg - m1 - th * m2)


def send_dt(n, me, q, ri, rk, dt_send, dt_chan, rows, cl, sems):
    ssem, rsem, lsem = sems

    def src(peer):
        return dt_send.at[pl.ds(peer * cl, cl), ri, rk]

    def dst(dev):
        return dt_chan.at[:, pl.ds(pl.multiple_of(dev * rows + ri.start, RB), RB), rk]

    pltpu.make_async_copy(src(me), dst(me), lsem).start()
    scatter(n, me, src, dst, ssem.at[q], rsem.at[q])


def finish_dt(n, nq, dt_chan, rows, sems):
    ssem, rsem, lsem = sems
    drain(dt_chan.at[:, pl.ds(0, rows), :], lsem)
    part = dt_chan.at[:, pl.ds(0, RB * (n - 1)), pl.ds(0, KB)]

    def one(q, carry):
        drain(part, ssem.at[q])
        drain(part, rsem.at[q])
        return carry

    lax.fori_loop(0, nq, one, 0)


def turn_kernel(n, ab_hbm, z_hbm, x_hbm, g_hbm, gq_ref, wo_ref, wg_ref,
                z_out, dg_out, dt_chan, gwo_ref, glq_ref,
                ab_v, z_v, x_v, g_v, dg_v, t_send, t_recv, t_v, dt_send, s_ref, isem, osem, tss, trs, ssem, rsem, lsem):
    rows, cols, c = z_v.shape
    cl = c // n
    nq = (rows // RB) * (cols // KB)
    loads = [pltpu.make_async_copy(a, b, isem.at[k]) for k, (a, b) in enumerate(((ab_hbm, ab_v), (z_hbm, z_v), (x_hbm, x_v), (g_hbm, g_v)))]
    for ld in loads:
        ld.start()
    gwo_ref[...] = jnp.zeros_like(gwo_ref)
    glq_ref[...] = jnp.zeros_like(glq_ref)
    me = enter(n)
    loads[0].wait()

    def tri(k, carry):
        t_send[k, :, :] = dot(ab_v[0, k], ab_v[1, k], 0, 0).astype(BF16)
        return carry

    lax.fori_loop(0, cl, tri, 0)
    send_t(n, me, nq, cols, t_send, t_recv, rows, cl, tss, trs)
    for ld in loads[1:]:
        ld.wait()
    sems = (ssem, rsem, lsem)

    def step(q, carry):
        ri, rk, i0 = block(q, cols)
        drain(t_recv.at[pl.ds(0, c - cl), ri, rk], trs.at[q])

        def write_t(sl, val):
            t_v[:, sl, :] = val

        unpack(lambda sl: t_recv[sl, ri, rk], c, write_t)

        def row(i, carry2):
            r = i0 + i
            th, rstd = norm(t_v[i].astype(F32), 0)
            y = (th * gq_ref[0] + gq_ref[1]).astype(BF16)
            upd = dot(y, wo_ref[...], 0, 0)
            gate = jax.nn.sigmoid(dot(x_v[r, rk, :], wg_ref[...], 1, 0))
            z_v[r, rk, :] = (z_v[r, rk, :].astype(F32) + gate * upd).astype(BF16)
            finish_back(i, r, rk, g_v[r, rk, :].astype(F32), th, rstd, y, upd, gate, gq_ref, wo_ref, dg_v, s_ref, gwo_ref, glq_ref)
            return carry2

        lax.fori_loop(0, RB, row, 0)

        def write(sl, val):
            dt_send[sl, ri, rk] = val

        pack(s_ref, 0, c, write)
        send_dt(n, me, q, ri, rk, dt_send, dt_chan, rows, cl, sems)
        pltpu.make_async_copy(z_v.at[ri, rk, :], z_out.at[ri, rk, :], osem.at[0]).start()
        pltpu.make_async_copy(dg_v.at[ri, rk, :], dg_out.at[ri, rk, :], osem.at[1]).start()
        return carry

    lax.fori_loop(0, nq, step, 0)
    drain(z_v, osem.at[0])
    drain(dg_v, osem.at[1])

    def sent(q, carry):
        drain(t_recv.at[pl.ds(0, c - cl), pl.ds(0, RB), pl.ds(0, KB)], tss.at[q])
        return carry

    lax.fori_loop(0, nq, sent, 0)
    finish_dt(n, nq, dt_chan, rows, sems)


def send_dab(n, me, nq, cols, ab_v, dab_recv, rows, cl, ssem, rsem):
    def one(q, carry):
        ri, rk, i0 = block(q, cols)

        def src(peer):
            return ab_v.at[:, :, pl.ds(pl.multiple_of(peer * rows + i0, RB), RB), rk]

        def dst(dev):
            return dab_recv.at[:, pl.ds(dev * cl, cl), ri, rk]

        scatter(n, me, src, dst, ssem.at[q], rsem.at[q])
        return carry

    lax.fori_loop(0, nq, one, 0)

    def own(k, carry):
        for h in range(2):
            dab_recv[h, me * cl + k, :, :] = ab_v[h, k, pl.ds(pl.multiple_of(me * rows, RB), rows), :]
        return carry

    lax.fori_loop(0, cl, own, 0)


def tri_back(cl, incoming, ab_v, dt_v):
    def one(k, carry):
        left, right, dt = ab_v[0, k], ab_v[1, k], dt_v[k]
        if incoming:
            d_left = dot(right, dt, 1, 1)
            d_right = dot(left, dt, 1, 0)
        else:
            d_left = dot(dt, right, 1, 0)
            d_right = dot(dt, left, 0, 0)
        ab_v[0, k, :, :] = d_left.astype(BF16)
        ab_v[1, k, :, :] = d_right.astype(BF16)
        return carry

    lax.fori_loop(0, cl, one, 0)


def project_back(i, r, rk, dab_t, m_ref, x_v, z_v, dg_v, dn_v, gp_ref, wpt_ref, wp_ref, wg_ref, gwp_ref, gwg_ref, glp_ref, c):
    x_row = x_v[r, rk, :]
    m_row = m_ref[pl.ds(r, 1), rk]
    p = dot(wpt_ref[...], x_row, 1, 1)
    parts = []
    for h in range(2):
        d_val = dab_t[i, h * c:(h + 1) * c, :].astype(F32) * m_row
        lin = p[2 * h * c:(2 * h + 1) * c]
        sig = jax.nn.sigmoid(p[(2 * h + 1) * c:(2 * h + 2) * c])
        d_lin = d_val * sig
        parts.append(d_lin.astype(BF16))
        parts.append((d_lin * lin * (1.0 - sig)).astype(BF16))
    d_proj = jnp.concatenate(parts, axis=0)
    d_gate = dg_v[r, rk, :]
    gwp_ref[...] += dot(d_proj, x_row, 1, 0)
    gwg_ref[...] += dot(x_row, d_gate, 0, 0)
    dxt = dot(wp_ref[...], d_proj, 1, 0) + dot(wg_ref[...], d_gate, 1, 1)
    dx = dxt.T.astype(BF16).astype(F32)
    xh, rstd = norm(z_v[r, rk, :].astype(F32), -1)
    glp_ref[0] += fold_rows(dx * xh)
    glp_ref[1] += fold_rows(dx)
    dxg = dx * gp_ref[0:1, :]
    m1 = jnp.mean(dxg, axis=-1, keepdims=True)
    m2 = jnp.mean(dxg * xh, axis=-1, keepdims=True)
    return (dn_v[r, rk, :].astype(F32) + rstd * (dxg - m1 - xh * m2)).astype(BF16)


def back_kernel(n, ab_hbm, dt_hbm, z_hbm, x_hbm, dg_hbm, dn_hbm, t_hbm, xp_hbm, m_ref, gp_ref, wpt_ref, wp_ref, wg_ref, gq_ref, wo_ref, wgp_ref,
                dn_out, dg_out, dt_chan, gwp_ref, gwg_ref, glp_ref, gwo_ref, glq_ref,
                ab_v, dt_v, z_v, x_v, dg_v, dn_v, t_v, xp_v, dab_recv, dab_t, dt_send, s_ref, isem, osem, tss, trs, ssem, rsem, lsem):
    rows, cols, c = z_v.shape
    cl = c // n
    nq = (rows // RB) * (cols // KB)
    pairs = ((ab_hbm, ab_v), (dt_hbm, dt_v), (z_hbm, z_v), (x_hbm, x_v), (dg_hbm, dg_v), (dn_hbm, dn_v), (t_hbm, t_v), (xp_hbm, xp_v))
    loads = [pltpu.make_async_copy(a, b, isem.at[k]) for k, (a, b) in enumerate(pairs)]
    for ld in loads:
        ld.start()
    for ref in (gwp_ref, gwg_ref, glp_ref, gwo_ref, glq_ref):
        ref[...] = jnp.zeros_like(ref)
    me = enter(n)
    loads[0].wait()
    loads[1].wait()
    tri_back(cl, True, ab_v, dt_v)
    send_dab(n, me, nq, cols, ab_v, dab_recv, rows, cl, tss, trs)
    for ld in loads[2:]:
        ld.wait()
    sems = (ssem, rsem, lsem)

    def step(q, carry):
        ri, rk, i0 = block(q, cols)
        drain(dab_recv.at[:, pl.ds(0, c - cl), ri, rk], trs.at[q])
        for h in range(2):
            def write_t(sl, val, h=h):
                dab_t[:, pl.ds(pl.multiple_of(h * c + sl.start, 16), 16), :] = val
            unpack(lambda sl, h=h: dab_recv[h, sl, ri, rk], c, write_t)

        def row(i, carry2):
            r = i0 + i
            dn = project_back(i, r, rk, dab_t, m_ref, x_v, z_v, dg_v, dn_v, gp_ref, wpt_ref, wp_ref, wg_ref, gwp_ref, gwg_ref, glp_ref, c)
            dn_v[r, rk, :] = dn
            th, rstd = norm(t_v[r, :, rk].astype(F32), 0)
            y = (th * gq_ref[0] + gq_ref[1]).astype(BF16)
            upd = dot(y, wo_ref[...], 0, 0)
            gate = jax.nn.sigmoid(dot(xp_v[r, rk, :], wgp_ref[...], 1, 0))
            finish_back(i, r, rk, dn.astype(F32), th, rstd, y, upd, gate, gq_ref, wo_ref, dg_v, s_ref, gwo_ref, glq_ref)
            return carry2

        lax.fori_loop(0, RB, row, 0)

        def write(sl, val):
            dt_send[sl, ri, rk] = val

        pack(s_ref, 0, c, write)
        send_dt(n, me, q, ri, rk, dt_send, dt_chan, rows, cl, sems)
        pltpu.make_async_copy(dn_v.at[ri, rk, :], dn_out.at[ri, rk, :], osem.at[0]).start()
        pltpu.make_async_copy(dg_v.at[ri, rk, :], dg_out.at[ri, rk, :], osem.at[1]).start()
        return carry

    lax.fori_loop(0, nq, step, 0)
    drain(dn_v, osem.at[0])
    drain(dg_v, osem.at[1])

    def sent(q, carry):
        drain(dab_recv.at[:, pl.ds(0, c - cl), pl.ds(0, RB), pl.ds(0, KB)], tss.at[q])
        return carry

    lax.fori_loop(0, nq, sent, 0)
    finish_dt(n, nq, dt_chan, rows, sems)


def last_kernel(n, ab_hbm, dt_hbm, z_hbm, x_hbm, dg_hbm, dn_hbm, m_ref, gp_ref, wpt_ref, wp_ref, wg_ref,
                dn_out, gwp_ref, gwg_ref, glp_ref,
                ab_v, dt_v, z_v, x_v, dg_v, dn_v, dab_recv, dab_t, isem, osem, tss, trs):
    rows, cols, c = z_v.shape
    cl = c // n
    nq = (rows // RB) * (cols // KB)
    pairs = ((ab_hbm, ab_v), (dt_hbm, dt_v), (z_hbm, z_v), (x_hbm, x_v), (dg_hbm, dg_v), (dn_hbm, dn_v))
    loads = [pltpu.make_async_copy(a, b, isem.at[k]) for k, (a, b) in enumerate(pairs)]
    for ld in loads:
        ld.start()
    for ref in (gwp_ref, gwg_ref, glp_ref):
        ref[...] = jnp.zeros_like(ref)
    me = enter(n)
    loads[0].wait()
    loads[1].wait()
    tri_back(cl, False, ab_v, dt_v)
    send_dab(n, me, nq, cols, ab_v, dab_recv, rows, cl, tss, trs)
    for ld in loads[2:]:
        ld.wait()

    def step(q, carry):
        ri, rk, i0 = block(q, cols)
        drain(dab_recv.at[:, pl.ds(0, c - cl), ri, rk], trs.at[q])
        for h in range(2):
            def write_t(sl, val, h=h):
                dab_t[:, pl.ds(pl.multiple_of(h * c + sl.start, 16), 16), :] = val
            unpack(lambda sl, h=h: dab_recv[h, sl, ri, rk], c, write_t)

        def row(i, carry2):
            r = i0 + i
            dn_v[r, rk, :] = project_back(i, r, rk, dab_t, m_ref, x_v, z_v, dg_v, dn_v, gp_ref, wpt_ref, wp_ref, wg_ref, gwp_ref, gwg_ref, glp_ref, c)
            return carry2

        lax.fori_loop(0, RB, row, 0)
        pltpu.make_async_copy(dn_v.at[ri, rk, :], dn_out.at[ri, rk, :], osem).start()
        return carry

    lax.fori_loop(0, nq, step, 0)
    drain(dn_v, osem)

    def sent(q, carry):
        drain(dab_recv.at[:, pl.ds(0, c - cl), pl.ds(0, RB), pl.ds(0, KB)], tss.at[q])
        return carry

    lax.fori_loop(0, nq, sent, 0)


def solution(mesh):
    row_spec = P(('data', AXIS), None, None)
    mask_spec = P(('data', AXIS), None)
    grad_spec = P('data', None, None)
    n = mesh.shape[AXIS]

    def device_step(z0, pair_mask, g, ln_pair, w_proj, w_gate, ln_chan, w_out):
        rows, cols, c = z0.shape
        cl = c // n
        nq = (rows // RB) * (cols // KB)
        mask_f = pair_mask.astype(F32)
        gp = ln_pair.astype(F32)
        gq = jnp.broadcast_to(ln_chan.astype(F32)[:, :, :, None], (2, 2, c, KB))
        wpt = jnp.swapaxes(w_proj, 1, 2)
        row_t = jax.ShapeDtypeStruct((rows, cols, c), BF16)
        t_row = jax.ShapeDtypeStruct((rows, c, cols), BF16)
        ab_t = jax.ShapeDtypeStruct((2, cl, cols, cols), BF16)
        dt_t = jax.ShapeDtypeStruct((cl, cols, cols), BF16)
        vm = pltpu.VMEM
        row_v = vm((rows, cols, c), BF16)
        ab_v = vm((2, cl, cols, cols), BF16)
        ab_rows = vm((2, c, rows, cols), BF16)
        t_c = vm((cl, cols, cols), BF16)
        t_rows = vm((c, rows, cols), BF16)
        dma = pltpu.SemaphoreType.DMA
        sq = dma((nq,))

        def call(body, cid, ins, outs, scratch, name):
            return pl.pallas_call(
                functools.partial(body, n),
                out_shape=tuple(o[0] for o in outs),
                in_specs=[s for _, s in ins],
                out_specs=tuple(o[1] for o in outs),
                scratch_shapes=scratch,
                compiler_params=pltpu.CompilerParams(collective_id=cid, has_side_effects=True, vmem_limit_bytes=63 * 1024 * 1024),
                name=name,
            )(*[a for a, _ in ins])

        def f32_out(*shape):
            return (jax.ShapeDtypeStruct(shape, F32), VM)

        x0, ab0 = call(first_kernel, 1,
                       [(z0, ANY), (mask_f, VM), (gp[0], VM), (wpt[0], VM)],
                       [(row_t, ANY), (ab_t, ANY)],
                       [row_v, row_v, ab_rows, vm((RB, 2 * c, KB), F32), dma, dma, sq, sq, dma], 'first')
        z1, x1, t0, ab1 = call(mid_kernel, 2,
                               [(ab0, ANY), (z0, ANY), (x0, ANY), (mask_f, VM), (gq[0], VM), (w_out[0], VM), (w_gate[0], VM), (gp[1], VM), (wpt[1], VM)],
                               [(row_t, ANY), (row_t, ANY), (t_row, ANY), (ab_t, ANY)],
                               [ab_v, row_v, row_v, t_c, t_rows, vm((rows, c, cols), BF16), ab_rows, vm((RB, 2 * c, KB), F32), dma((3,)), dma((3,)), sq, sq, sq, sq, dma], 'mid')
        z2, dg1, dt1, gwo1, glq1 = call(turn_kernel, 3,
                                        [(ab1, ANY), (z1, ANY), (x1, ANY), (g, ANY), (gq[1], VM), (w_out[1], VM), (w_gate[1], VM)],
                                        [(row_t, ANY), (row_t, ANY), (dt_t, ANY), f32_out(c, c), f32_out(2, c, 128)],
                                        [ab_v, row_v, row_v, row_v, row_v, t_c, t_rows, vm((RB, c, KB), BF16), t_rows, vm((RB, c, KB), F32), dma((4,)), dma((2,)), sq, sq, sq, sq, dma], 'turn')
        dmid, dg0, dt0, gwp1, gwg1, glp1, gwo0, glq0 = call(back_kernel, 4,
                                                            [(ab1, ANY), (dt1, ANY), (z1, ANY), (x1, ANY), (dg1, ANY), (g, ANY), (t0, ANY), (x0, ANY), (mask_f, VM), (gp[1], VM), (wpt[1], VM), (w_proj[1], VM), (w_gate[1], VM), (gq[0], VM), (w_out[0], VM), (w_gate[0], VM)],
                                                            [(row_t, ANY), (row_t, ANY), (dt_t, ANY), f32_out(4 * c, c), f32_out(c, c), f32_out(2, 8, c), f32_out(c, c), f32_out(2, c, 128)],
                                                            [ab_v, t_c, row_v, row_v, row_v, row_v, vm((rows, c, cols), BF16), row_v, ab_rows, vm((RB, 2 * c, KB), BF16), t_rows, vm((RB, c, KB), F32), dma((8,)), dma((2,)), sq, sq, sq, sq, dma], 'back')
        dz, gwp0, gwg0, glp0 = call(last_kernel, 5,
                                    [(ab0, ANY), (dt0, ANY), (z0, ANY), (x0, ANY), (dg0, ANY), (dmid, ANY), (mask_f, VM), (gp[0], VM), (wpt[0], VM), (w_proj[0], VM), (w_gate[0], VM)],
                                    [(row_t, ANY), f32_out(4 * c, c), f32_out(c, c), f32_out(2, 8, c)],
                                    [ab_v, t_c, row_v, row_v, row_v, row_v, ab_rows, vm((RB, 2 * c, KB), BF16), dma((6,)), dma, sq, sq], 'last')
        local = (jnp.stack([glp0.sum(1), glp1.sum(1)]), jnp.stack([gwp0, gwp1]), jnp.stack([gwg0, gwg1]), jnp.stack([glq0.sum(2), glq1.sum(2)]), jnp.stack([gwo0, gwo1]))
        tot = lax.psum(local, AXIS)
        tot = (tot[0], jnp.swapaxes(tot[1], 1, 2)) + tuple(tot[2:])
        return (z2, dz) + tuple(v.astype(BF16) for v in tot)

    full = P()
    return jax.shard_map(device_step, mesh=mesh, in_specs=(row_spec, mask_spec, row_spec, full, full, full, full, full), out_specs=(row_spec, row_spec, grad_spec, grad_spec, grad_spec, grad_spec, grad_spec), check_vma=False)
```

time: 1720 us -> 1280 us (0.74)
  Pallas kernels: 0 us -> 1200 us
  blocking collectives: 646 us -> 54.5 us
  waiting for transfers between devices: 462 us -> 0 us
  other arithmetic: 221 us -> 5.65 us
  matrix products: 175 us -> 0 us
  local copies, waits for them, and re-layouts: 186 us -> 14.8 us
  starting transfers between devices: 20.4 us -> 0 us
    pallas_call x0 -> x5, Pallas kernels: none -> 1200 us  [call(): pl.pallas_call(functools.partial(body, n), out_shape=tuple((o[0] for o in...]
    all_to_all x4 -> x0, blocking collectives: 594 us -> none  [to_channels(): lax.all_to_all(row_blocks, GROUP_AXIS, chan_dim, chan_dim + 1, tiled=True)]
    all_to_all x4 -> x0, waiting for transfers between devices: 462 us -> none  [to_rows(): lax.all_to_all(chan_blocks, GROUP_AXIS, chan_dim + 1, chan_dim, tiled=True)]
    dot_general x24 -> x0, matrix products: 175 us -> none  [the longest x2 26.6 us: update_forward(): jnp.einsum('ijd,de->eij', x_norm, w_proj, preferred_element_type=jnp.floa...]
    another operation x17 -> x5, other arithmetic: 98.6 us -> 1.86 us  [the longest x1 0.99 us: device_step(): jnp.stack([gwp0, gwp1])]
    convert_element_type x12 -> x3, other arithmetic: 66.7 us -> 2.84 us  [the longest x1 1.47 us: device_step(): mask_f = pair_mask.astype(F32)]
    convert_element_type x10 -> x0, local copies, waits for them, and re-layouts: 58.3 us -> none  [the longest x4 32.9 us: update_forward(): t_rows.astype(jnp.float32)]
    reduce_sum x13 -> x4, other arithmetic: 55.4 us -> 0.95 us  [the longest x1 0.71 us: device_step(): glp0.sum(1)]
  transfers between devices with their start and end apart: 4 -> 0, of which waited for: 4 -> 0; matrix products, arithmetic and copies ran while one was open for 6% -> 0% of each run, Pallas kernels for 0% -> 0%
where the time goes in v1:
time: 1280 us; the launch traced here: 1270 us
  Pallas kernels  1200 us (94%)
  blocking collectives  54.5 us (4%)
  local copies, waits for them, and re-layouts  14.8 us (1%)
    pallas_call x5, Pallas kernels, call(): pl.pallas_call(functools.partial(body, n), out_shape=tuple((o[0] for o in...  1200 us
    psum x1, blocking collectives, device_step(): tot = lax.psum(local, AXIS)  54.5 us

profile of v1, /device:TPU:23, one launch (start us, length us, event | category | flops | bytes accessed | tf_op | source)
XLA Modules:
  0.0 1271.7 jit_solution(10952326107431291763)
XLA Ops:
  0.6 0.7 convert_element_type.28
  1.3 0.6 slice_bitcast_fusion.9
  1.9 0.7 convert_element_type.29
  2.6 1.5 convert_element_type.27.m_ref
  4.0 1.5 slice_bitcast_fusion.4
  5.5 0.8 broadcast_in_dim.15.gq_ref
  6.3 0.8 broadcast_in_dim.13.gq_ref
  7.1 1.1 copy.15
  8.2 0.7 slice_bitcast_fusion
  8.9 1.7 slice_bitcast_fusion.2
  10.6 203.4 %first.1 = (bf16[32,512,128]{2,1,0:T(8,128)(2,1)}, bf16[2,8,512,512]{3,2,1,0:T(8,128)(2,1)}) custom-call(bf16[32,512,128]{2,1,0:T(8,128)(2,1)} %z_hbm.5, f32[32,512]{1,0:T(8,128)} %convert_element_type.27.m_ref, f32[2,128]{1,0:T(2,128)} %get-tuple-element.76.gp_ref, bf16[512,128]{1,0:T(8,128)(2,1)} %get-tuple-element.68.wpt_ref), custom_call_target="tpu_custom_call" | custom-call | tf_op jit(solution)/shard_map/first/pallas_call | solution.py:566
  214.1 284.0 %mid.1 = (bf16[32,512,128]{2,1,0:T(8,128)(2,1)}, bf16[32,512,128]{2,1,0:T(8,128)(2,1)}, bf16[32,128,512]{2,1,0:T(8,128)(2,1)}, bf16[2,8,512,512]{3,2,1,0:T(8,128)(2,1)}) custom-call(bf16[2,8,512,512]{3,2,1,0:T(8,128)(2,1)} %get-tuple-element.30.ab_hbm, bf16[32,512,128]{2,1,0:T(8,128)(2,1)} %z_hbm.5, bf16[32,512,128]{2,1,0:T(8,128)(2,1)} %get-tuple-element.31.x_hbm.xp_hbm, ...), custom_call_target="tpu_custom_call" | custom-call | tf_op jit(solution)/shard_map/mid/pallas_call | solution.py:566
  498.1 202.3 %turn.1 = (bf16[32,512,128]{2,1,0:T(8,128)(2,1)}, bf16[32,512,128]{2,1,0:T(8,128)(2,1)}, bf16[8,512,512]{2,1,0:T(8,128)(2,1)}, f32[128,128]{1,0:T(8,128)}, f32[2,128,128]{2,1,0:T(8,128)}) custom-call(bf16[2,8,512,512]{3,2,1,0:T(8,128)(2,1)} %get-tuple-element.32.ab_hbm, bf16[32,512,128]{2,1,0:T(8,128)(2,1)} %get-tuple-element.33.z_hbm, ...), custom_call_target="tpu_custom_call" | custom-call | tf_op jit(solution)/shard_map/turn/pallas_call | solution.py:566
  700.4 291.9 %back.1 = (bf16[32,512,128]{2,1,0:T(8,128)(2,1)}, bf16[32,512,128]{2,1,0:T(8,128)(2,1)}, bf16[8,512,512]{2,1,0:T(8,128)(2,1)}, f32[512,128]{1,0:T(8,128)}, f32[1...) custom-call(bf16[2,8,512,512]{3,2,1,0:T(8,128)(2,1)} %get-tuple-element.32.ab_hbm, ...), custom_call_target="tpu_custom_call" | custom-call | tf_op jit(solution)/shard_map/back/pallas_call | solution.py:566
  992.3 214.3 %last.1 = (bf16[32,512,128]{2,1,0:T(8,128)(2,1)}, f32[512,128]{1,0:T(8,128)}, f32[128,128]{1,0:T(8,128)}, f32[2,8,128]{2,1,0:T(8,128)}) custom-call(bf16[2,8,512,512]{3,2,1,0:T(8,128)(2,1)} %get-tuple-element.30.ab_hbm, bf16[8,512,512]{2,1,0:T(8,128)(2,1)} %get-tuple-element.39.dt_hbm, bf16[32,512,128]{2,1,0:T(8,128)(2,1)} %z_hbm.5, ...), custom_call_target="tpu_custom_call" | custom-call | tf_op jit(solution)/shard_map/last/pallas_call | solution.py:566
  1206.6 0.7 reduce_sum.36
  1207.4 0.1 reduce_sum.38
  1207.5 0.1 reduce_sum.39
  1207.6 0.9 pad_maximum_fusion.1
  1208.5 1.0 pad_maximum_fusion
  1209.5 54.5 %all-reduce.2 = (bf16[2,2,128]{2,1,0:T(2,128)(2,1)}, bf16[2,512,128]{2,1,0:T(8,128)(2,1)S(1)}, bf16[2,128,128]{2,1,0:T(8,128)(2,1)}, bf16[2,2,128]{2,1,0:T(2,128)(2,1)}, bf16[2,128,128]{2,1,0:T(8,128)(2,1)}) all-reduce(f32[2,2,128]{2,1,0:T(2,128)S(1)} %pad_maximum_fusion.3, ...), channel_id=1, replica_groups=mesh['data'=4,'dap'=16] {'dap'}, use_global_device_ids=true, to_apply=%region_2.0 | all-reduce | flops 197632 | bytes 1185792 | tf_op jit(solution)/shard_map/psum | solution.py:600
  1264.1 0.8 copy.16
  1264.9 4.8 copy.29
  1269.7 2.0 copy.30
  (21 shorter events, 0.1 us)
Async XLA Ops:
  992.3 215.1 %copy-start.7 = (f32[2,8,128]{2,1,0:T(8,128)S(1)}, f32[2,8,128]{2,1,0:T(8,128)}, u32[]{:S(2)}) copy-start(f32[2,8,128]{2,1,0:T(8,128)} %get-tuple-element.44) | copy-start | bytes 24580
  992.3 215.1 %copy-start.3 = (f32[2,128,128]{2,1,0:T(8,128)S(1)}, f32[2,128,128]{2,1,0:T(8,128)}, u32[]{:S(2)}) copy-start(f32[2,128,128]{2,1,0:T(8,128)} %get-tuple-element.49) | copy-start | bytes 393220
  992.3 215.2 %copy-start.2 = (f32[2,128,128]{2,1,0:T(8,128)S(1)}, f32[2,128,128]{2,1,0:T(8,128)}, u32[]{:S(2)}) copy-start(f32[2,128,128]{2,1,0:T(8,128)} %get-tuple-element.50) | copy-start | bytes 393220
  992.3 215.3 %copy-start.6 = (f32[128,128]{1,0:T(8,128)S(1)}, f32[128,128]{1,0:T(8,128)}, u32[]{:S(2)}) copy-start(f32[128,128]{1,0:T(8,128)} %get-tuple-element.48) | copy-start | bytes 196612
  992.3 216.2 %copy-start.4 = (f32[128,128]{1,0:T(8,128)S(1)}, f32[128,128]{1,0:T(8,128)}, u32[]{:S(2)}) copy-start(f32[128,128]{1,0:T(8,128)} %get-tuple-element.52) | copy-start | bytes 196612
  992.3 216.2 %copy-start.5 = (f32[128,128]{1,0:T(8,128)S(1)}, f32[128,128]{1,0:T(8,128)}, u32[]{:S(2)}) copy-start(f32[128,128]{1,0:T(8,128)} %get-tuple-element.51) | copy-start | bytes 196612
  992.3 216.2 %copy-start.1 = (f32[512,128]{1,0:T(8,128)S(1)}, f32[512,128]{1,0:T(8,128)}, u32[]{:S(2)}) copy-start(f32[512,128]{1,0:T(8,128)} %get-tuple-element.46) | copy-start | bytes 786436
  1264.9 4.8 copy-start

commit v2 on v1

v2 whole, which is shorter than its diff:
```python
import functools

import jax
import jax.numpy as jnp
from jax import lax
from jax.experimental import pallas as pl
from jax.experimental.pallas import tpu as pltpu
from jax.sharding import PartitionSpec as P

LN_EPS = 1e-5
AXIS = 'dap'
F32 = jnp.float32
BF16 = jnp.bfloat16
RB = 16
KB = 256
KB_EDGE = 128
UNROLL = 2
MESH_ID = pl.DeviceIdType.MESH
ANY = pl.BlockSpec(memory_space=pl.ANY)
VM = pl.BlockSpec(memory_space=pltpu.VMEM)


def dot(lhs, rhs, lc, rc):
    return lax.dot_general(lhs, rhs, (((lc,), (rc,)), ((), ())), preferred_element_type=F32)


def norm(values, axis):
    mean = jnp.mean(values, axis=axis, keepdims=True)
    cent = values - mean
    var = jnp.mean(cent * cent, axis=axis, keepdims=True)
    rstd = lax.rsqrt(var + LN_EPS)
    return cent * rstd, rstd


def greet(n):
    me = lax.axis_index(AXIS)
    bar = pltpu.get_barrier_semaphore()

    def one(s, carry):
        pl.semaphore_signal(bar, inc=1, device_id={AXIS: lax.rem(me + s, n)}, device_id_type=MESH_ID)
        return carry

    lax.fori_loop(1, n, one, 0)
    return me


def meet(n):
    pl.semaphore_wait(pltpu.get_barrier_semaphore(), n - 1)


def scatter(n, me, src, dst, ssem, rsem):
    def one(s, carry):
        peer = lax.rem(me + s, n)
        pltpu.make_async_remote_copy(src_ref=src(peer), dst_ref=dst(me), send_sem=ssem, recv_sem=rsem, device_id={AXIS: peer}, device_id_type=MESH_ID).start()
        return carry

    lax.fori_loop(1, n, one, 0)


def drain(ref, sem):
    pltpu.make_async_copy(ref, ref, sem).wait()


def drain_all(nq, part, *sems):
    def one(q, carry):
        for sem in sems:
            drain(part, sem.at[q])
        return carry

    lax.fori_loop(0, nq, one, 0)


def block(q, cols, kb):
    per = cols // kb
    i0 = pl.multiple_of((q // per) * RB, RB)
    k0 = pl.multiple_of(lax.rem(q, per) * kb, kb)
    return pl.ds(i0, RB), pl.ds(k0, kb), i0


def pair_params(u, lnp_ref):
    return lnp_ref[u, 0:1, :].astype(F32), lnp_ref[u, 1:2, :].astype(F32)


def load_wpt(u, wp_ref, wpt_v):
    wpt_v[...] = wp_ref[u].astype(F32).T.astype(BF16)


def load_mask(m_ref, m_v):
    for r in range(m_v.shape[0]):
        m_v[r, 0:1, :] = m_ref[r:r + 1, :].astype(F32)


def load_chan(u, lnq_ref, gq_v):
    c = gq_v.shape[1]
    for h in range(2):
        row = lnq_ref[u, h:h + 1, :].astype(F32)
        col = jnp.broadcast_to(row, (128, c)).T
        for l in range(gq_v.shape[2] // 128):
            gq_v[h, :, l * 128:(l + 1) * 128] = col


def pack(s_ref, e0, count, write):
    def one(e, carry):
        off = pl.multiple_of(e * 8, 8)
        val = s_ref[:, pl.ds(e0 + off, 8), :]
        write(pl.ds(off, 8), jnp.swapaxes(val, 0, 1).astype(BF16))
        return carry

    lax.fori_loop(0, count // 8, one, 0)


def unpack(read, count, write):
    def one(e, carry):
        sl = pl.ds(pl.multiple_of(e * 16, 16), 16)
        write(sl, jnp.swapaxes(read(sl).astype(F32), 0, 1).astype(BF16))
        return carry

    lax.fori_loop(0, count // 16, one, 0)


def each_row(row):
    lax.fori_loop(0, RB, row, 0, unroll=UNROLL)


def project(s_ref, i, x_row, m_row, wpt_v, c):
    p = dot(wpt_v[...], x_row, 1, 1)
    s_ref[i, 0:c, :] = m_row * jax.nn.sigmoid(p[c:2 * c]) * p[0:c]
    s_ref[i, c:2 * c, :] = m_row * jax.nn.sigmoid(p[3 * c:]) * p[2 * c:3 * c]


def fold_rows(v):
    return jnp.sum(v.reshape(v.shape[0] // 8, 8, v.shape[1]), axis=0)


def fold_lanes(v):
    out = v[:, 0:128]
    for h in range(1, v.shape[1] // 128):
        out = out + v[:, h * 128:(h + 1) * 128]
    return out


def send_ab(n, me, q, ri, rk, ab_send, ab_chan, rows, cl, sems):
    ssem, rsem, lsem = sems

    def src(peer):
        return ab_send.at[:, pl.ds(peer * cl, cl), ri, rk]

    def dst(dev):
        return ab_chan.at[:, :, pl.ds(pl.multiple_of(dev * rows + ri.start, RB), RB), rk]

    pltpu.make_async_copy(src(me), dst(me), lsem).start()
    scatter(n, me, src, dst, ssem.at[q], rsem.at[q])


def finish_ab(n, nq, kb, ab_chan, rows, sems):
    ssem, rsem, lsem = sems
    drain(ab_chan.at[:, :, pl.ds(0, rows), :], lsem)
    drain_all(nq, ab_chan.at[:, :, pl.ds(0, RB * (n - 1)), pl.ds(0, kb)], ssem, rsem)


def pack_ab(s_ref, c, ab_send, ri, rk):
    for h in range(2):
        def write(sl, val, h=h):
            ab_send[h, sl, ri, rk] = val
        pack(s_ref, h * c, c, write)


def first_kernel(n, z_hbm, m_ref, lnp_ref, wp_ref, x_out, ab_chan, z_v, x_v, ab_send, s_ref, wpt_v, m_v, isem, osem, ssem, rsem, lsem):
    rows, cols, c = z_v.shape
    cl = c // n
    kb = KB_EDGE
    nq = (rows // RB) * (cols // kb)
    load = pltpu.make_async_copy(z_hbm, z_v, isem)
    load.start()
    me = greet(n)
    load_wpt(0, wp_ref, wpt_v)
    load_mask(m_ref, m_v)
    gain, shift = pair_params(0, lnp_ref)
    load.wait()
    sems = (ssem, rsem, lsem)

    def step(q, carry):
        ri, rk, i0 = block(q, cols, kb)

        def row(i, carry2):
            r = i0 + i
            xh, _ = norm(z_v[r, rk, :].astype(F32), -1)
            x_row = (xh * gain + shift).astype(BF16)
            x_v[r, rk, :] = x_row
            project(s_ref, i, x_row, m_v[r, 0:1, rk], wpt_v, c)
            return carry2

        each_row(row)
        pack_ab(s_ref, c, ab_send, ri, rk)

        @pl.when(q == 0)
        def _():
            meet(n)

        send_ab(n, me, q, ri, rk, ab_send, ab_chan, rows, cl, sems)
        pltpu.make_async_copy(x_v.at[ri, rk, :], x_out.at[ri, rk, :], osem).start()
        return carry

    lax.fori_loop(0, nq, step, 0)
    drain(x_v, osem)
    finish_ab(n, nq, kb, ab_chan, rows, sems)


def exchange_t(n, me, nq, cols, kb, product, t_send, t_recv, rows, cl, ssem, rsem):
    def send(k0, count, q):
        ri, rk, i0 = block(q, cols, kb)

        def src(peer):
            return t_send.at[pl.ds(k0, count), pl.ds(pl.multiple_of(peer * rows + i0, RB), RB), rk]

        def dst(dev):
            return t_recv.at[pl.ds(dev * cl + k0, count), ri, rk]

        scatter(n, me, src, dst, ssem.at[q], rsem.at[q])

    def one(k, carry):
        product(k)

        @pl.when(k == 0)
        def _():
            meet(n)

        send(k, 1, 0)
        return carry

    lax.fori_loop(0, cl, one, 0)

    def rest(q, carry):
        send(0, cl, q)
        return carry

    lax.fori_loop(1, nq, rest, 0)

    def own(k, carry):
        t_recv[me * cl + k, :, :] = t_send[k, pl.ds(pl.multiple_of(me * rows, RB), rows), :]
        return carry

    lax.fori_loop(0, cl, own, 0)


def start_loads(chan_pairs, row_pairs, csem, isem):
    cl = csem.shape[1]
    chan = []
    for h, (src, dst) in enumerate(chan_pairs):
        def cut(k, src=src, dst=dst, h=h):
            return pltpu.make_async_copy(src(k), dst(k), csem.at[h, k])
        chan.append(cut)

    def one(k, carry):
        for cut in chan:
            cut(k).start()
        return carry

    lax.fori_loop(0, cl, one, 0)
    loads = [pltpu.make_async_copy(a, b, isem.at[j]) for j, (a, b) in enumerate(row_pairs)]
    for ld in loads:
        ld.start()

    def wait_chan(k):
        for cut in chan:
            cut(k).wait()

    def wait_rows():
        for ld in loads:
            ld.wait()

    return wait_chan, wait_rows


def mid_kernel(n, ab_hbm, z_hbm, x_hbm, m_ref, lnp_ref, wp_ref, wg_ref, lnq_ref, wo_ref,
               z_out, x_out, t_out, ab_chan,
               ab_v, z_v, x_v, t_send, t_recv, t_v, ab_send, s_ref, wpt_v, m_v, gq_v, csem, isem, osem, tss, trs, ssem, rsem, lsem):
    rows, cols, c = z_v.shape
    cl = c // n
    kb = KB
    nq = (rows // RB) * (cols // kb)
    wait_chan, wait_rows = start_loads([(lambda k: ab_hbm.at[:, k], lambda k: ab_v.at[:, k])], [(z_hbm, z_v), (x_hbm, x_v)], csem, isem)
    me = greet(n)
    load_wpt(1, wp_ref, wpt_v)
    load_mask(m_ref, m_v)
    load_chan(0, lnq_ref, gq_v)
    gain, shift = pair_params(1, lnp_ref)

    def product(k):
        wait_chan(k)
        t_send[k, :, :] = dot(ab_v[0, k], ab_v[1, k], 1, 1).astype(BF16)

    exchange_t(n, me, nq, cols, kb, product, t_send, t_recv, rows, cl, tss, trs)
    wait_rows()
    sems = (ssem, rsem, lsem)

    def step(q, carry):
        ri, rk, i0 = block(q, cols, kb)
        drain(t_recv.at[pl.ds(0, c - cl), ri, rk], trs.at[q])

        def write_t(sl, val):
            t_v[ri, sl, rk] = val

        unpack(lambda sl: t_recv[sl, ri, rk], c, write_t)

        def row(i, carry2):
            r = i0 + i
            th, _ = norm(t_v[r, :, rk].astype(F32), 0)
            y = (th * gq_v[0] + gq_v[1]).astype(BF16)
            upd = dot(y, wo_ref[0], 0, 0)
            gate = jax.nn.sigmoid(dot(x_v[r, rk, :], wg_ref[0], 1, 0))
            z_new = (z_v[r, rk, :].astype(F32) + gate * upd).astype(BF16)
            z_v[r, rk, :] = z_new
            xh, _ = norm(z_new.astype(F32), -1)
            x_row = (xh * gain + shift).astype(BF16)
            x_v[r, rk, :] = x_row
            project(s_ref, i, x_row, m_v[r, 0:1, rk], wpt_v, c)
            return carry2

        each_row(row)
        pack_ab(s_ref, c, ab_send, ri, rk)
        send_ab(n, me, q, ri, rk, ab_send, ab_chan, rows, cl, sems)
        pltpu.make_async_copy(z_v.at[ri, rk, :], z_out.at[ri, rk, :], osem.at[0]).start()
        pltpu.make_async_copy(x_v.at[ri, rk, :], x_out.at[ri, rk, :], osem.at[1]).start()
        pltpu.make_async_copy(t_v.at[ri, :, rk], t_out.at[ri, :, rk], osem.at[2]).start()
        return carry

    lax.fori_loop(0, nq, step, 0)
    drain(z_v, osem.at[0])
    drain(x_v, osem.at[1])
    drain(t_v, osem.at[2])
    drain_all(nq, t_recv.at[pl.ds(0, c - cl), pl.ds(0, RB), pl.ds(0, kb)], tss)
    finish_ab(n, nq, kb, ab_chan, rows, sems)


def finish_back(i, r, rk, dn, th, rstd, y, upd, gate, gq_v, w_out, dg_v, s_ref, gwo_ref, glq_ref):
    d_gate = dn * upd * gate * (1.0 - gate)
    d_upd = (dn * gate).astype(BF16)
    dg_v[r, rk, :] = d_gate.astype(BF16)
    gwo_ref[...] += dot(y, d_upd, 1, 0)
    dy = dot(w_out, d_upd, 1, 1).astype(BF16).astype(F32)
    glq_ref[0] += fold_lanes(dy * th)
    glq_ref[1] += fold_lanes(dy)
    dyg = dy * gq_v[0]
    m1 = jnp.mean(dyg, axis=0, keepdims=True)
    m2 = jnp.mean(dyg * th, axis=0, keepdims=True)
    s_ref[i] = rstd * (dyg - m1 - th * m2)


def send_dt(n, me, q, ri, rk, dt_send, dt_chan, rows, cl, sems):
    ssem, rsem, lsem = sems

    def src(peer):
        return dt_send.at[pl.ds(peer * cl, cl), ri, rk]

    def dst(dev):
        return dt_chan.at[:, pl.ds(pl.multiple_of(dev * rows + ri.start, RB), RB), rk]

    pltpu.make_async_copy(src(me), dst(me), lsem).start()
    scatter(n, me, src, dst, ssem.at[q], rsem.at[q])


def finish_dt(n, nq, kb, dt_chan, rows, sems):
    ssem, rsem, lsem = sems
    drain(dt_chan.at[:, pl.ds(0, rows), :], lsem)
    drain_all(nq, dt_chan.at[:, pl.ds(0, RB * (n - 1)), pl.ds(0, kb)], ssem, rsem)


def turn_kernel(n, ab_hbm, z_hbm, x_hbm, g_hbm, wg_ref, lnq_ref, wo_ref,
                z_out, dg_out, dt_chan, gwo_ref, glq_ref,
                ab_v, z_v, x_v, g_v, dg_v, t_send, t_recv, t_v, dt_send, s_ref, gq_v, csem, isem, osem, tss, trs, ssem, rsem, lsem):
    rows, cols, c = z_v.shape
    cl = c // n
    kb = KB
    nq = (rows // RB) * (cols // kb)
    wait_chan, wait_rows = start_loads([(lambda k: ab_hbm.at[:, k], lambda k: ab_v.at[:, k])], [(z_hbm, z_v), (x_hbm, x_v), (g_hbm, g_v)], csem, isem)
    me = greet(n)
    gwo_ref[...] = jnp.zeros_like(gwo_ref)
    glq_ref[...] = jnp.zeros_like(glq_ref)
    load_chan(1, lnq_ref, gq_v)

    def product(k):
        wait_chan(k)
        t_send[k, :, :] = dot(ab_v[0, k], ab_v[1, k], 0, 0).astype(BF16)

    exchange_t(n, me, nq, cols, kb, product, t_send, t_recv, rows, cl, tss, trs)
    wait_rows()
    sems = (ssem, rsem, lsem)

    def step(q, carry):
        ri, rk, i0 = block(q, cols, kb)
        drain(t_recv.at[pl.ds(0, c - cl), ri, rk], trs.at[q])

        def write_t(sl, val):
            t_v[:, sl, :] = val

        unpack(lambda sl: t_recv[sl, ri, rk], c, write_t)

        def row(i, carry2):
            r = i0 + i
            th, rstd = norm(t_v[i].astype(F32), 0)
            y = (th * gq_v[0] + gq_v[1]).astype(BF16)
            upd = dot(y, wo_ref[1], 0, 0)
            gate = jax.nn.sigmoid(dot(x_v[r, rk, :], wg_ref[1], 1, 0))
            z_v[r, rk, :] = (z_v[r, rk, :].astype(F32) + gate * upd).astype(BF16)
            finish_back(i, r, rk, g_v[r, rk, :].astype(F32), th, rstd, y, upd, gate, gq_v, wo_ref[1], dg_v, s_ref, gwo_ref, glq_ref)
            return carry2

        each_row(row)

        def write(sl, val):
            dt_send[sl, ri, rk] = val

        pack(s_ref, 0, c, write)
        send_dt(n, me, q, ri, rk, dt_send, dt_chan, rows, cl, sems)
        pltpu.make_async_copy(z_v.at[ri, rk, :], z_out.at[ri, rk, :], osem.at[0]).start()
        pltpu.make_async_copy(dg_v.at[ri, rk, :], dg_out.at[ri, rk, :], osem.at[1]).start()
        return carry

    lax.fori_loop(0, nq, step, 0)
    drain(z_v, osem.at[0])
    drain(dg_v, osem.at[1])
    drain_all(nq, t_recv.at[pl.ds(0, c - cl), pl.ds(0, RB), pl.ds(0, kb)], tss)
    finish_dt(n, nq, kb, dt_chan, rows, sems)


def exchange_dab(n, me, nq, cols, kb, incoming, wait_chan, ab_v, dt_v, dab_recv, rows, cl, ssem, rsem, between):
    def send(k0, count, q):
        ri, rk, i0 = block(q, cols, kb)

        def src(peer):
            return ab_v.at[:, pl.ds(k0, count), pl.ds(pl.multiple_of(peer * rows + i0, RB), RB), rk]

        def dst(dev):
            return dab_recv.at[:, pl.ds(dev * cl + k0, count), ri, rk]

        scatter(n, me, src, dst, ssem.at[q], rsem.at[q])

    def one(k, carry):
        wait_chan(k)
        left, right, dt = ab_v[0, k], ab_v[1, k], dt_v[k]
        if incoming:
            d_left = dot(right, dt, 1, 1)
            d_right = dot(left, dt, 1, 0)
        else:
            d_left = dot(dt, right, 1, 0)
            d_right = dot(dt, left, 0, 0)
        ab_v[0, k, :, :] = d_left.astype(BF16)
        ab_v[1, k, :, :] = d_right.astype(BF16)

        @pl.when(k == 0)
        def _():
            between()

        send(k, 1, 0)
        return carry

    lax.fori_loop(0, cl, one, 0)

    def rest(q, carry):
        send(0, cl, q)
        return carry

    lax.fori_loop(1, nq, rest, 0)

    def own(k, carry):
        for h in range(2):
            dab_recv[h, me * cl + k, :, :] = ab_v[h, k, pl.ds(pl.multiple_of(me * rows, RB), rows), :]
        return carry

    lax.fori_loop(0, cl, own, 0)


def unpack_dab(dab_recv, dab_t, c, ri, rk):
    for h in range(2):
        def write_t(sl, val, h=h):
            dab_t[:, pl.ds(pl.multiple_of(h * c + sl.start, 16), 16), :] = val
        unpack(lambda sl, h=h: dab_recv[h, sl, ri, rk], c, write_t)


def project_back(u, i, r, rk, dab_t, m_v, x_v, z_v, dg_v, dn_v, gain, wpt_v, wp_ref, wg_ref, gwp_ref, gwg_ref, glp_ref, c):
    x_row = x_v[r, rk, :]
    m_row = m_v[r, 0:1, rk]
    p = dot(wpt_v[...], x_row, 1, 1)
    parts = []
    for h in range(2):
        d_val = dab_t[i, h * c:(h + 1) * c, :].astype(F32) * m_row
        lin = p[2 * h * c:(2 * h + 1) * c]
        sig = jax.nn.sigmoid(p[(2 * h + 1) * c:(2 * h + 2) * c])
        d_lin = d_val * sig
        parts.append(d_lin.astype(BF16))
        parts.append((d_lin * lin * (1.0 - sig)).astype(BF16))
    d_proj = jnp.concatenate(parts, axis=0)
    d_gate = dg_v[r, rk, :]
    gwp_ref[...] += dot(d_proj, x_row, 1, 0)
    gwg_ref[...] += dot(x_row, d_gate, 0, 0)
    dxt = dot(wp_ref[u], d_proj, 1, 0) + dot(wg_ref[u], d_gate, 1, 1)
    dx = dxt.T.astype(BF16).astype(F32)
    xh, rstd = norm(z_v[r, rk, :].astype(F32), -1)
    glp_ref[0] += fold_rows(dx * xh)
    glp_ref[1] += fold_rows(dx)
    dxg = dx * gain
    m1 = jnp.mean(dxg, axis=-1, keepdims=True)
    m2 = jnp.mean(dxg * xh, axis=-1, keepdims=True)
    return (dn_v[r, rk, :].astype(F32) + rstd * (dxg - m1 - xh * m2)).astype(BF16)


def back_kernel(n, ab_hbm, dt_hbm, z_hbm, x_hbm, dg_hbm, dn_hbm, t_hbm, xp_hbm, m_ref, lnp_ref, wp_ref, wg_ref, lnq_ref, wo_ref,
                dn_out, dg_out, dt_chan, gwp_ref, gwg_ref, glp_ref, gwo_ref, glq_ref,
                ab_v, dt_v, z_v, x_v, dg_v, dn_v, t_v, xp_v, dab_recv, dab_t, dt_send, s_ref, wpt_v, m_v, gq_v, csem, isem, osem, tss, trs, ssem, rsem, lsem):
    rows, cols, c = z_v.shape
    cl = c // n
    kb = KB
    nq = (rows // RB) * (cols // kb)
    chan = [(lambda k: ab_hbm.at[:, k], lambda k: ab_v.at[:, k]), (lambda k: dt_hbm.at[k], lambda k: dt_v.at[k])]
    wait_chan, wait_rows = start_loads(chan, [(z_hbm, z_v), (x_hbm, x_v), (dg_hbm, dg_v), (dn_hbm, dn_v), (t_hbm, t_v), (xp_hbm, xp_v)], csem, isem)
    me = greet(n)
    for ref in (gwp_ref, gwg_ref, glp_ref, gwo_ref, glq_ref):
        ref[...] = jnp.zeros_like(ref)
    load_wpt(1, wp_ref, wpt_v)
    load_mask(m_ref, m_v)
    load_chan(0, lnq_ref, gq_v)
    gain, _ = pair_params(1, lnp_ref)
    exchange_dab(n, me, nq, cols, kb, True, wait_chan, ab_v, dt_v, dab_recv, rows, cl, tss, trs, lambda: meet(n))
    wait_rows()
    sems = (ssem, rsem, lsem)

    def step(q, carry):
        ri, rk, i0 = block(q, cols, kb)
        drain(dab_recv.at[:, pl.ds(0, c - cl), ri, rk], trs.at[q])
        unpack_dab(dab_recv, dab_t, c, ri, rk)

        def row(i, carry2):
            r = i0 + i
            dn = project_back(1, i, r, rk, dab_t, m_v, x_v, z_v, dg_v, dn_v, gain, wpt_v, wp_ref, wg_ref, gwp_ref, gwg_ref, glp_ref, c)
            dn_v[r, rk, :] = dn
            th, rstd = norm(t_v[r, :, rk].astype(F32), 0)
            y = (th * gq_v[0] + gq_v[1]).astype(BF16)
            upd = dot(y, wo_ref[0], 0, 0)
            gate = jax.nn.sigmoid(dot(xp_v[r, rk, :], wg_ref[0], 1, 0))
            finish_back(i, r, rk, dn.astype(F32), th, rstd, y, upd, gate, gq_v, wo_ref[0], dg_v, s_ref, gwo_ref, glq_ref)
            return carry2

        each_row(row)

        def write(sl, val):
            dt_send[sl, ri, rk] = val

        pack(s_ref, 0, c, write)
        send_dt(n, me, q, ri, rk, dt_send, dt_chan, rows, cl, sems)
        pltpu.make_async_copy(dn_v.at[ri, rk, :], dn_out.at[ri, rk, :], osem.at[0]).start()
        pltpu.make_async_copy(dg_v.at[ri, rk, :], dg_out.at[ri, rk, :], osem.at[1]).start()
        return carry

    lax.fori_loop(0, nq, step, 0)
    drain(dn_v, osem.at[0])
    drain(dg_v, osem.at[1])
    drain_all(nq, dab_recv.at[:, pl.ds(0, c - cl), pl.ds(0, RB), pl.ds(0, kb)], tss)
    finish_dt(n, nq, kb, dt_chan, rows, sems)


def add_parts(n, recv):
    def one(s, acc):
        return acc + recv[s]

    return lax.fori_loop(1, n, one, recv[0])


def last_kernel(n, ab_hbm, dt_hbm, z_hbm, x_hbm, dg_hbm, dn_hbm, m_ref, lnp_ref, wp_ref, wg_ref,
                gwp1_ref, gwg1_ref, gwo1_ref, gwo0_ref, glp1_ref, glq1_ref, glq0_ref,
                dn_out, grads_out, small_out,
                ab_v, dt_v, z_v, x_v, dg_v, dn_v, dab_recv, dab_t, wpt_v, m_v, gwp_ref, gwg_ref, glp_ref, early, early_in, late, late_in, mine,
                csem, isem, osem, tss, trs, gss, grs, lsem):
    rows, cols, c = z_v.shape
    cl = c // n
    kb = KB_EDGE
    nq = (rows // RB) * (cols // kb)
    we, wc = 4 * c // n, c // n
    chan = [(lambda k: ab_hbm.at[:, k], lambda k: ab_v.at[:, k]), (lambda k: dt_hbm.at[k], lambda k: dt_v.at[k])]
    wait_chan, wait_rows = start_loads(chan, [(z_hbm, z_v), (x_hbm, x_v), (dg_hbm, dg_v), (dn_hbm, dn_v)], csem, isem)
    me = greet(n)
    for ref in (gwp_ref, gwg_ref, glp_ref):
        ref[...] = jnp.zeros_like(ref)
    load_wpt(0, wp_ref, wpt_v)
    load_mask(m_ref, m_v)
    gain, _ = pair_params(0, lnp_ref)
    small = [jnp.sum(glp1_ref[h], axis=0, keepdims=True) for h in range(2)]
    small += [jnp.sum(ref[h].T, axis=0, keepdims=True) for ref in (glq1_ref, glq0_ref) for h in range(2)]
    small = jnp.concatenate(small + [jnp.zeros((2, c), F32)], axis=0)
    e1, e2, e3, e4 = we, we + wc, we + 2 * wc, we + 3 * wc

    def fill(p, carry):
        early[p, 0:e1, :] = gwp1_ref[pl.ds(pl.multiple_of(p * we, 8), we), :]
        cut = pl.ds(pl.multiple_of(p * wc, 8), wc)
        early[p, e1:e2, :] = gwg1_ref[cut, :]
        early[p, e2:e3, :] = gwo1_ref[cut, :]
        early[p, e3:e4, :] = gwo0_ref[cut, :]
        early[p, e4:e4 + 8, :] = small
        return carry

    lax.fori_loop(0, n, fill, 0)
    early_in[me] = early[me]

    def between():
        meet(n)

    exchange_dab(n, me, nq, cols, kb, False, wait_chan, ab_v, dt_v, dab_recv, rows, cl, tss, trs, between)
    scatter(n, me, lambda p: early.at[p], lambda d: early_in.at[d], gss.at[0], grs.at[0])
    wait_rows()

    def step(q, carry):
        ri, rk, i0 = block(q, cols, kb)
        drain(dab_recv.at[:, pl.ds(0, c - cl), ri, rk], trs.at[q])
        unpack_dab(dab_recv, dab_t, c, ri, rk)

        def row(i, carry2):
            r = i0 + i
            dn_v[r, rk, :] = project_back(0, i, r, rk, dab_t, m_v, x_v, z_v, dg_v, dn_v, gain, wpt_v, wp_ref, wg_ref, gwp_ref, gwg_ref, glp_ref, c)
            return carry2

        each_row(row)
        pltpu.make_async_copy(dn_v.at[ri, rk, :], dn_out.at[ri, rk, :], osem).start()
        return carry

    lax.fori_loop(0, nq, step, 0)
    tail = jnp.concatenate([jnp.sum(glp_ref[h], axis=0, keepdims=True) for h in range(2)] + [jnp.zeros((6, c), F32)], axis=0)

    def fill_late(p, carry):
        late[p, 0:e1, :] = gwp_ref[pl.ds(pl.multiple_of(p * we, 8), we), :]
        late[p, e1:e2, :] = gwg_ref[pl.ds(pl.multiple_of(p * wc, 8), wc), :]
        late[p, e2:e2 + 8, :] = tail
        return carry

    lax.fori_loop(0, n, fill_late, 0)
    late_in[me] = late[me]
    scatter(n, me, lambda p: late.at[p], lambda d: late_in.at[d], gss.at[1], grs.at[1])
    part = early.at[pl.ds(0, n - 1)]
    drain(part, grs.at[0])
    sum_e = add_parts(n, early_in)
    part_l = late.at[pl.ds(0, n - 1)]
    drain(part_l, grs.at[1])
    sum_l = add_parts(n, late_in)
    mine[...] = jnp.concatenate([sum_e[0:e1], sum_l[0:e1], sum_e[e1:e4], sum_l[e1:e2]], axis=0).astype(BF16)
    small_out[0:8, :] = sum_e[e4:e4 + 8]
    small_out[8:16, :] = sum_l[e2:e2 + 8]
    own = pltpu.make_async_copy(mine, grads_out.at[me], lsem)
    own.start()
    scatter(n, me, lambda p: mine, lambda d: grads_out.at[d], gss.at[2], grs.at[2])
    drain(dn_v, osem)
    drain_all(nq, dab_recv.at[:, pl.ds(0, c - cl), pl.ds(0, RB), pl.ds(0, kb)], tss)
    drain(part, gss.at[0])
    drain(part_l, gss.at[1])
    own.wait()
    gathered = grads_out.at[pl.ds(0, n - 1)]
    drain(gathered, gss.at[2])
    drain(gathered, grs.at[2])


def solution(mesh):
    row_spec = P(('data', AXIS), None, None)
    mask_spec = P(('data', AXIS), None)
    grad_spec = P('data', None, None)
    n = mesh.shape[AXIS]

    def device_step(z0, mask, g, ln_pair, w_proj, w_gate, ln_chan, w_out):
        rows, cols, c = z0.shape
        cl = c // n
        nq = (rows // RB) * (cols // KB)
        ne = (rows // RB) * (cols // KB_EDGE)
        row_t = jax.ShapeDtypeStruct((rows, cols, c), BF16)
        t_row = jax.ShapeDtypeStruct((rows, c, cols), BF16)
        ab_t = jax.ShapeDtypeStruct((2, cl, cols, cols), BF16)
        dt_t = jax.ShapeDtypeStruct((cl, cols, cols), BF16)
        vm = pltpu.VMEM
        row_v = vm((rows, cols, c), BF16)
        ab_v = vm((2, cl, cols, cols), BF16)
        ab_rows = vm((2, c, rows, cols), BF16)
        t_c = vm((cl, cols, cols), BF16)
        t_rows = vm((c, rows, cols), BF16)
        wpt_v = vm((4 * c, c), BF16)
        gq_v = vm((2, c, KB), F32)
        m_v = vm((rows, 1, cols), F32)
        dma = pltpu.SemaphoreType.DMA
        sq, se = dma((nq,)), dma((ne,))

        def call(body, cid, ins, outs, scratch, name):
            return pl.pallas_call(
                functools.partial(body, n),
                out_shape=tuple(o[0] for o in outs),
                in_specs=[s for _, s in ins],
                out_specs=tuple(o[1] for o in outs),
                scratch_shapes=scratch,
                compiler_params=pltpu.CompilerParams(collective_id=cid, has_side_effects=True, vmem_limit_bytes=63 * 1024 * 1024),
                name=name,
            )(*[a for a, _ in ins])

        def f32_out(*shape):
            return (jax.ShapeDtypeStruct(shape, F32), VM)

        mk, lnp, wp, wg, lnq, wo = ((v, VM) for v in (mask, ln_pair, w_proj, w_gate, ln_chan, w_out))
        x0, ab0 = call(first_kernel, 1, [(z0, ANY), mk, lnp, wp], [(row_t, ANY), (ab_t, ANY)],
                       [row_v, row_v, ab_rows, vm((RB, 2 * c, KB_EDGE), F32), wpt_v, m_v, dma, dma, se, se, dma], 'first')
        z1, x1, t0, ab1 = call(mid_kernel, 2, [(ab0, ANY), (z0, ANY), (x0, ANY), mk, lnp, wp, wg, lnq, wo],
                               [(row_t, ANY), (row_t, ANY), (t_row, ANY), (ab_t, ANY)],
                               [ab_v, row_v, row_v, t_c, t_rows, vm((rows, c, cols), BF16), ab_rows, vm((RB, 2 * c, KB), F32), wpt_v, m_v, gq_v, dma((1, cl)), dma((2,)), dma((3,)), sq, sq, sq, sq, dma], 'mid')
        z2, dg1, dt1, gwo1, glq1 = call(turn_kernel, 3, [(ab1, ANY), (z1, ANY), (x1, ANY), (g, ANY), wg, lnq, wo],
                                        [(row_t, ANY), (row_t, ANY), (dt_t, ANY), f32_out(c, c), f32_out(2, c, 128)],
                                        [ab_v, row_v, row_v, row_v, row_v, t_c, t_rows, vm((RB, c, KB), BF16), t_rows, vm((RB, c, KB), F32), gq_v, dma((1, cl)), dma((3,)), dma((2,)), sq, sq, sq, sq, dma], 'turn')
        dmid, dg0, dt0, gwp1, gwg1, glp1, gwo0, glq0 = call(
            back_kernel, 4, [(ab1, ANY), (dt1, ANY), (z1, ANY), (x1, ANY), (dg1, ANY), (g, ANY), (t0, ANY), (x0, ANY), mk, lnp, wp, wg, lnq, wo],
            [(row_t, ANY), (row_t, ANY), (dt_t, ANY), f32_out(4 * c, c), f32_out(c, c), f32_out(2, 8, c), f32_out(c, c), f32_out(2, c, 128)],
            [ab_v, t_c, row_v, row_v, row_v, row_v, vm((rows, c, cols), BF16), row_v, ab_rows, vm((RB, 2 * c, KB), BF16), t_rows, vm((RB, c, KB), F32), wpt_v, m_v, gq_v, dma((2, cl)), dma((6,)), dma((2,)), sq, sq, sq, sq, dma], 'back')
        we, wc = 4 * c // n, c // n
        er, lr, gr = we + 3 * wc + 8, we + wc + 8, 2 * we + 4 * wc
        dz, grads, small = call(
            last_kernel, 5,
            [(ab0, ANY), (dt0, ANY), (z0, ANY), (x0, ANY), (dg0, ANY), (dmid, ANY), mk, lnp, wp, wg] + [(v, VM) for v in (gwp1, gwg1, gwo1, gwo0, glp1, glq1, glq0)],
            [(row_t, ANY), (jax.ShapeDtypeStruct((n, gr, c), BF16), ANY), f32_out(16, c)],
            [ab_v, t_c, row_v, row_v, row_v, row_v, ab_rows, vm((RB, 2 * c, KB_EDGE), BF16), wpt_v, m_v, vm((4 * c, c), F32), vm((c, c), F32), vm((2, 8, c), F32)]
            + [vm((n, k, c), F32) for k in (er, er, lr, lr)] + [vm((gr, c), BF16), dma((2, cl)), dma((4,)), dma, se, se, dma((3,)), dma((3,)), dma], 'last')

        def rows_of(start, count):
            return grads[:, start:start + count].reshape(n * count, c)

        base = 2 * we
        d_wp = jnp.stack([rows_of(we, we).T, rows_of(0, we).T])
        d_wg = jnp.stack([rows_of(base + 3 * wc, wc), rows_of(base, wc)])
        d_wo = jnp.stack([rows_of(base + 2 * wc, wc), rows_of(base + wc, wc)])
        small = small.astype(BF16)
        d_lp = jnp.stack([small[8:10], small[0:2]])
        d_lq = jnp.stack([small[4:6], small[2:4]])
        return z2, dz, d_lp, d_wp, d_wg, d_lq, d_wo

    full = P()
    return jax.shard_map(device_step, mesh=mesh, in_specs=(row_spec, mask_spec, row_spec, full, full, full, full, full), out_specs=(row_spec, row_spec, grad_spec, grad_spec, grad_spec, grad_spec, grad_spec), check_vma=False)
```

time: 1280 us -> 1210 us (0.945)
  blocking collectives: 54.5 us -> 0 us
    psum x1 -> x0, blocking collectives: 54.5 us -> none  [device_step(): tot = lax.psum(local, AXIS)]
where the time goes in v2:
time: 1210 us
  Pallas kernels  1190 us (98%)
    pallas_call x5, Pallas kernels, call(): pl.pallas_call(functools.partial(body, n), out_shape=tuple((o[0] for o in...  1190 us

profile of v2, /device:TPU:23, one launch (start us, length us, event | category | flops | bytes accessed | tf_op | source)
XLA Modules:
  0.0 1205.4 jit_solution(9899361288506196665)
XLA Ops:
  0.6 197.8 %first.1 = (bf16[32,512,128]{2,1,0:T(8,128)(2,1)}, bf16[2,8,512,512]{3,2,1,0:T(8,128)(2,1)}) custom-call(bf16[32,512,128]{2,1,0:T(8,128)(2,1)} %z_hbm.5, s32[32,512]{1,0:T(8,128)} %m_ref.7, bf16[2,2,128]{2,1,0:T(2,128)(2,1)} %lnp_ref.7, bf16[2,128,512]{2,1,0:T(8,128)(2,1)} %wp_ref.7), custom_call_target="tpu_custom_call" | custom-call | tf_op jit(solution)/shard_map/first/pallas_call | solution.py:687
  198.5 285.5 %mid.1 = (bf16[32,512,128]{2,1,0:T(8,128)(2,1)}, bf16[32,512,128]{2,1,0:T(8,128)(2,1)}, bf16[32,128,512]{2,1,0:T(8,128)(2,1)}, bf16[2,8,512,512]{3,2,1,0:T(8,128)(2,1)}) custom-call(bf16[2,8,512,512]{3,2,1,0:T(8,128)(2,1)} %get-tuple-element.29.ab_hbm, bf16[32,512,128]{2,1,0:T(8,128)(2,1)} %z_hbm.5, bf16[32,512,128]{2,1,0:T(8,128)(2,1)} %get-tuple-element.30.x_hbm.xp_hbm, ...), custom_call_target="tpu_custom_call" | custom-call | tf_op jit(solution)/shard_map/mid/pallas_call | solution.py:687
  484.0 189.4 %turn.1 = (bf16[32,512,128]{2,1,0:T(8,128)(2,1)}, bf16[32,512,128]{2,1,0:T(8,128)(2,1)}, bf16[8,512,512]{2,1,0:T(8,128)(2,1)}, f32[128,128]{1,0:T(8,128)}, f32[2,128,128]{2,1,0:T(8,128)}) custom-call(bf16[2,8,512,512]{3,2,1,0:T(8,128)(2,1)} %get-tuple-element.31.ab_hbm, bf16[32,512,128]{2,1,0:T(8,128)(2,1)} %get-tuple-element.32.z_hbm, ...), custom_call_target="tpu_custom_call" | custom-call | tf_op jit(solution)/shard_map/turn/pallas_call | solution.py:687
  673.4 293.1 %back.1 = (bf16[32,512,128]{2,1,0:T(8,128)(2,1)}, bf16[32,512,128]{2,1,0:T(8,128)(2,1)}, bf16[8,512,512]{2,1,0:T(8,128)(2,1)}, f32[512,128]{1,0:T(8,128)}, f32[1...) custom-call(bf16[2,8,512,512]{3,2,1,0:T(8,128)(2,1)} %get-tuple-element.31.ab_hbm, ...), custom_call_target="tpu_custom_call" | custom-call | tf_op jit(solution)/shard_map/back/pallas_call | solution.py:687
  966.5 227.3 %last.1 = (bf16[32,512,128]{2,1,0:T(8,128)(2,1)}, bf16[16,96,128]{2,1,0:T(8,128)(2,1)}, f32[16,128]{1,0:T(8,128)}) custom-call(bf16[2,8,512,512]{3,2,1,0:T(8,128)(2,1)} %get-tuple-element.29.ab_hbm, bf16[8,512,512]{2,1,0:T(8,128)(2,1)} %get-tuple-element.38.dt_hbm, bf16[32,512,128]{2,1,0:T(8,128)(2,1)} %z_hbm.5, ...), custom_call_target="tpu_custom_call" | custom-call | tf_op jit(solution)/shard_map/last/pallas_call | solution.py:687
  1193.9 0.7 convert_element_type.3
  1194.6 0.6 pad_maximum_fusion.3
  1195.1 0.8 slice_bitcast_fusion.1
  1196.0 1.0 fusion
  1197.0 0.1 copy.15
  1197.1 0.1 copy.16
  1197.2 0.7 pad_maximum_fusion
  1197.9 0.7 pad_maximum_fusion.1
  1198.6 0.0 copy-start
  1198.6 4.8 copy.19
  1203.4 0.0 copy-done
  1203.4 2.0 copy.20
  (1 shorter events, 0.0 us)
Async XLA Ops:
  1198.6 4.8 copy-start

commit v3 on v0

v3 whole, which is shorter than its diff:
```python
import functools

import jax
import jax.numpy as jnp
from jax import lax
from jax.experimental import pallas as pl
from jax.experimental.pallas import tpu as pltpu
from jax.sharding import PartitionSpec as P

LN_EPS = 1e-5
AXIS = 'dap'
F32 = jnp.float32
BF16 = jnp.bfloat16
RB = 16
KB = 128
UNROLL = 2
MESH_ID = pl.DeviceIdType.MESH
ANY = pl.BlockSpec(memory_space=pl.ANY)
VM = pl.BlockSpec(memory_space=pltpu.VMEM)


def dot(lhs, rhs, lc, rc):
    return lax.dot_general(lhs, rhs, (((lc,), (rc,)), ((), ())), preferred_element_type=F32)


def norm(values, axis):
    mean = jnp.mean(values, axis=axis, keepdims=True)
    cent = values - mean
    var = jnp.mean(cent * cent, axis=axis, keepdims=True)
    rstd = lax.rsqrt(var + LN_EPS)
    return cent * rstd, rstd


def greet(n):
    me = lax.axis_index(AXIS)
    bar = pltpu.get_barrier_semaphore()

    def one(s, carry):
        pl.semaphore_signal(bar, inc=1, device_id={AXIS: lax.rem(me + s, n)}, device_id_type=MESH_ID)
        return carry

    lax.fori_loop(1, n, one, 0)
    return me


def meet(n):
    pl.semaphore_wait(pltpu.get_barrier_semaphore(), n - 1)


def scatter(n, me, src, dst, ssem, rsem):
    def one(s, carry):
        far = (s + 1) // 2
        peer = lax.rem(me + far * lax.rem(s, 2) + (n - far) * (1 - lax.rem(s, 2)), n)
        pltpu.make_async_remote_copy(src_ref=src(peer), dst_ref=dst(me), send_sem=ssem, recv_sem=rsem, device_id={AXIS: peer}, device_id_type=MESH_ID).start()
        return carry

    lax.fori_loop(1, n, one, 0)


def drain(ref, sem):
    pltpu.make_async_copy(ref, ref, sem).wait()


def drain_all(nq, part, sem):
    def one(q, carry):
        drain(part, sem(q))
        return carry

    lax.fori_loop(0, nq, one, 0)


def block(q, cols):
    per = cols // KB
    i0 = pl.multiple_of((q // per) * RB, RB)
    k0 = pl.multiple_of(lax.rem(q, per) * KB, KB)
    return pl.ds(i0, RB), pl.ds(k0, KB), i0


def pair_params(u, lnp_ref):
    return lnp_ref[u, 0:1, :].astype(F32), lnp_ref[u, 1:2, :].astype(F32)


def load_wpt(u, wp_ref, wpt_v):
    wpt_v[u] = wp_ref[u].astype(F32).T.astype(BF16)


def load_mask(m_ref, m_v):
    for r in range(m_v.shape[0]):
        m_v[r, 0:1, :] = m_ref[r:r + 1, :].astype(F32)


def load_chan(u, lnq_ref, gq_v):
    c = gq_v.shape[2]
    for h in range(2):
        row = lnq_ref[u, h:h + 1, :].astype(F32)
        col = jnp.broadcast_to(row, (128, c)).T
        for l in range(gq_v.shape[3] // 128):
            gq_v[u, h, :, l * 128:(l + 1) * 128] = col


def pack(s_ref, e0, count, write):
    def one(e, carry):
        off = pl.multiple_of(e * 8, 8)
        val = s_ref[:, pl.ds(e0 + off, 8), :]
        write(pl.ds(off, 8), jnp.swapaxes(val, 0, 1).astype(BF16))
        return carry

    lax.fori_loop(0, count // 8, one, 0)


def unpack(read, count, write):
    def one(e, carry):
        sl = pl.ds(pl.multiple_of(e * 16, 16), 16)
        write(sl, jnp.swapaxes(read(sl).astype(F32), 0, 1).astype(BF16))
        return carry

    lax.fori_loop(0, count // 16, one, 0)


def each_row(row):
    lax.fori_loop(0, RB, row, 0, unroll=UNROLL)


def project(s_ref, i, x_row, m_row, w_t, c):
    p = dot(w_t, x_row, 1, 1)
    s_ref[i, 0:c, :] = m_row * jax.nn.sigmoid(p[c:2 * c]) * p[0:c]
    s_ref[i, c:2 * c, :] = m_row * jax.nn.sigmoid(p[3 * c:]) * p[2 * c:3 * c]


def fold_rows(v):
    return jnp.sum(v.reshape(v.shape[0] // 8, 8, v.shape[1]), axis=0)


def fold_lanes(v):
    out = v[:, 0:128]
    for h in range(1, v.shape[1] // 128):
        out = out + v[:, h * 128:(h + 1) * 128]
    return out


def pack_ab(s_ref, c, abr, ri, rk):
    for h in range(2):
        def write(sl, val, h=h):
            abr[h, sl, ri, rk] = val
        pack(s_ref, h * c, c, write)


def unpack_dab(abr, dab_t, c, ri, rk):
    for h in range(2):
        def write_t(sl, val, h=h):
            dab_t[:, pl.ds(pl.multiple_of(h * c + sl.start, 16), 16), :] = val
        unpack(lambda sl, h=h: abr[h, sl, ri, rk], c, write_t)


def finish_back(i, r, rk, dn, th, rstd, y, upd, gate, gain, w_out, dg_v, s_ref, gwo, glq, u):
    d_gate = dn * upd * gate * (1.0 - gate)
    d_upd = (dn * gate).astype(BF16)
    dg_v[r, rk, :] = d_gate.astype(BF16)
    gwo[u] += dot(y, d_upd, 1, 0)
    dy = dot(w_out, d_upd, 1, 1).astype(BF16).astype(F32)
    glq[u, 0] += fold_lanes(dy * th)
    glq[u, 1] += fold_lanes(dy)
    dyg = dy * gain
    m1 = jnp.mean(dyg, axis=0, keepdims=True)
    m2 = jnp.mean(dyg * th, axis=0, keepdims=True)
    s_ref[i, 0:dy.shape[0], :] = rstd * (dyg - m1 - th * m2)


def project_back(u, i, r, rk, dab_t, m_v, x_v, z_v, dg_v, dn_v, gain, wpt_v, wp_ref, wg_ref, gwp, gwg, glp, c):
    x_row = x_v[r, rk, :]
    m_row = m_v[r, 0:1, rk]
    p = dot(wpt_v[u], x_row, 1, 1)
    parts = []
    for h in range(2):
        d_val = dab_t[i, h * c:(h + 1) * c, :].astype(F32) * m_row
        lin = p[2 * h * c:(2 * h + 1) * c]
        sig = jax.nn.sigmoid(p[(2 * h + 1) * c:(2 * h + 2) * c])
        d_lin = d_val * sig
        parts.append(d_lin.astype(BF16))
        parts.append((d_lin * lin * (1.0 - sig)).astype(BF16))
    d_proj = jnp.concatenate(parts, axis=0)
    d_gate = dg_v[r, rk, :]
    gwp[u] += dot(d_proj, x_row, 1, 0)
    gwg[u] += dot(x_row, d_gate, 0, 0)
    dxt = dot(wp_ref[u], d_proj, 1, 0) + dot(wg_ref[u], d_gate, 1, 1)
    dx = dxt.T.astype(BF16).astype(F32)
    xh, rstd = norm(z_v[r, rk, :].astype(F32), -1)
    glp[u, 0] += fold_rows(dx * xh)
    glp[u, 1] += fold_rows(dx)
    dxg = dx * gain
    m1 = jnp.mean(dxg, axis=-1, keepdims=True)
    m2 = jnp.mean(dxg * xh, axis=-1, keepdims=True)
    return (dn_v[r, rk, :].astype(F32) + rstd * (dxg - m1 - xh * m2)).astype(BF16)


def to_pair(n, me, src, dst, ssem, rsem):
    partner = me + 1 - 2 * lax.rem(me, 2)
    pltpu.make_async_remote_copy(src_ref=src, dst_ref=dst, send_sem=ssem, recv_sem=rsem, device_id={AXIS: partner}, device_id_type=MESH_ID).start()


def to_chips(n, me, src, dst, ssem, rsem):
    core, chip = lax.rem(me, 2), me // 2

    def one(s, carry):
        other = lax.rem(chip + s, n // 2)
        pltpu.make_async_remote_copy(src_ref=src(other), dst_ref=dst(chip), send_sem=ssem, recv_sem=rsem, device_id={AXIS: 2 * other + core}, device_id_type=MESH_ID).start()
        return carry

    lax.fori_loop(1, n // 2, one, 0)


def pair_sum(core, parts, pair_in, comb):
    def one(z, carry):
        comb[z] = parts[z, core] + pair_in[z]
        return carry

    lax.fori_loop(0, comb.shape[0], one, 0)


def add_parts(recv):
    def one(s, acc):
        return acc + recv[s]

    return lax.fori_loop(1, recv.shape[0], one, recv[0])


def whole_kernel(n, z_hbm, m_ref, g_hbm, lnp_ref, wp_ref, wg_ref, lnq_ref, wo_ref,
                 zo_hbm, dz_hbm, x0_hbm, t0_hbm, grads_ref, small_ref,
                 ab0, ab1, abr, ts, tr, dt, z_v, x_v, g_v, dg_v, s_ref, dab_t, t_c, xp_c, zo_c,
                 wpt_v, gq_v, m_v, gwp, gwg, gwo, glp, glq,
                 early, pair_e, comb_e, gath_e, late, pair_l, comb_l, gath_l, mine, all_v,
                 sems, isem, osem, gss, grs):
    rows, cols, c = z_v.shape
    cl = c // n
    nq = (rows // RB) * (cols // KB)
    we, wc = 4 * c // n, c // n
    load_z = pltpu.make_async_copy(z_hbm, z_v, isem.at[0])
    load_g = pltpu.make_async_copy(g_hbm, g_v, isem.at[1])
    load_z.start()
    load_g.start()
    me = greet(n)
    core, chip = lax.rem(me, 2), me // 2

    def snd(k):
        return lambda q: sems.at[k, 0, q]

    def rcv(k):
        return lambda q: sems.at[k, 1, q]

    ab_part = ab0.at[:, :, pl.ds(0, RB * (n - 1)), pl.ds(0, KB)]
    dt_part = dt.at[:, pl.ds(0, RB * (n - 1)), pl.ds(0, KB)]
    t_part = tr.at[pl.ds(0, c - cl), pl.ds(0, RB), pl.ds(0, KB)]
    dab_part = abr.at[:, pl.ds(0, c - cl), pl.ds(0, RB), pl.ds(0, KB)]

    def send_ab(k, q, dest):
        ri, rk, i0 = block(q, cols)

        def at(dev):
            return pl.ds(pl.multiple_of(dev * rows + i0, RB), RB)

        scatter(n, me, lambda p: abr.at[:, pl.ds(p * cl, cl), ri, rk], lambda d: dest.at[:, :, at(d), rk], snd(k)(q), rcv(k)(q))

        def own(j, carry):
            for h in range(2):
                dest[h, j, at(me), rk] = abr[h, me * cl + j, ri, rk]
            return carry

        lax.fori_loop(0, cl, own, 0)

    def send_dt(k, q):
        ri, rk, i0 = block(q, cols)

        def at(dev):
            return pl.ds(pl.multiple_of(dev * rows + i0, RB), RB)

        scatter(n, me, lambda p: tr.at[pl.ds(p * cl, cl), ri, rk], lambda d: dt.at[:, at(d), rk], snd(k)(q), rcv(k)(q))

        def own(j, carry):
            dt[j, at(me), rk] = tr[me * cl + j, ri, rk]
            return carry

        lax.fori_loop(0, cl, own, 0)

    def exchange(product, send):
        def one(j, carry):
            product(j)
            send(j, 1, 0)
            return carry

        lax.fori_loop(0, cl, one, 0)

        def rest(q, carry):
            send(0, cl, q)
            return carry

        lax.fori_loop(1, nq, rest, 0)

    def exchange_t(k, product):
        def send(j, count, q):
            ri, rk, i0 = block(q, cols)
            scatter(n, me, lambda p: ts.at[pl.ds(j, count), pl.ds(pl.multiple_of(p * rows + i0, RB), RB), rk], lambda d: tr.at[pl.ds(d * cl + j, count), ri, rk], snd(k)(q), rcv(k)(q))

        exchange(product, send)

        def own(j, carry):
            tr[me * cl + j, :, :] = ts[j, pl.ds(pl.multiple_of(me * rows, RB), rows), :]
            return carry

        lax.fori_loop(0, cl, own, 0)

    def exchange_dab(k, incoming, ab):
        def product(j):
            left, right, d_t = ab[0, j], ab[1, j], dt[j]
            if incoming:
                d_left = dot(right, d_t, 1, 1)
                d_right = dot(left, d_t, 1, 0)
            else:
                d_left = dot(d_t, right, 1, 0)
                d_right = dot(d_t, left, 0, 0)
            ab[0, j, :, :] = d_left.astype(BF16)
            ab[1, j, :, :] = d_right.astype(BF16)

        def send(j, count, q):
            ri, rk, i0 = block(q, cols)
            scatter(n, me, lambda p: ab.at[:, pl.ds(j, count), pl.ds(pl.multiple_of(p * rows + i0, RB), RB), rk], lambda d: abr.at[:, pl.ds(d * cl + j, count), ri, rk], snd(k)(q), rcv(k)(q))

        exchange(product, send)

        def own(j, carry):
            for h in range(2):
                abr[h, me * cl + j, :, :] = ab[h, j, pl.ds(pl.multiple_of(me * rows, RB), rows), :]
            return carry

        lax.fori_loop(0, cl, own, 0)

    load_wpt(0, wp_ref, wpt_v)
    load_mask(m_ref, m_v)
    gain0, shift0 = pair_params(0, lnp_ref)
    gain1, shift1 = pair_params(1, lnp_ref)
    load_z.wait()

    def step1(q, carry):
        ri, rk, i0 = block(q, cols)

        def row(i, carry2):
            r = i0 + i
            xh, _ = norm(z_v[r, rk, :].astype(F32), -1)
            x_row = (xh * gain0 + shift0).astype(BF16)
            x_v[r, rk, :] = x_row
            project(s_ref, i, x_row, m_v[r, 0:1, rk], wpt_v[0], c)
            return carry2

        each_row(row)
        pack_ab(s_ref, c, abr, ri, rk)

        @pl.when(q == 0)
        def _():
            meet(n)

        send_ab(0, q, ab0)
        pltpu.make_async_copy(x_v.at[ri, rk, :], x0_hbm.at[ri, rk, :], osem.at[0]).start()
        return carry

    lax.fori_loop(0, nq, step1, 0)
    load_wpt(1, wp_ref, wpt_v)
    for u in range(2):
        load_chan(u, lnq_ref, gq_v)
    for ref in (gwp, gwg, gwo, glp, glq):
        ref[...] = jnp.zeros_like(ref)
    drain(x_v, osem.at[0])
    drain_all(nq, ab_part, snd(0))
    drain_all(nq, ab_part, rcv(0))

    def product0(j):
        ts[j, :, :] = dot(ab0[0, j], ab0[1, j], 1, 1).astype(BF16)

    exchange_t(1, product0)

    def step2(q, carry):
        ri, rk, i0 = block(q, cols)

        @pl.when(q > 0)
        def _():
            drain(t_c, osem.at[1])

        drain(t_part, rcv(1)(q))

        def write_t(sl, val):
            t_c[:, sl, :] = val

        unpack(lambda sl: tr[sl, ri, rk], c, write_t)
        pltpu.make_async_copy(t_c, t0_hbm.at[ri, :, rk], osem.at[1]).start()

        def row(i, carry2):
            r = i0 + i
            th, _ = norm(t_c[i].astype(F32), 0)
            y = (th * gq_v[0, 0] + gq_v[0, 1]).astype(BF16)
            upd = dot(y, wo_ref[0], 0, 0)
            gate = jax.nn.sigmoid(dot(x_v[r, rk, :], wg_ref[0], 1, 0))
            z_new = (z_v[r, rk, :].astype(F32) + gate * upd).astype(BF16)
            z_v[r, rk, :] = z_new
            xh, _ = norm(z_new.astype(F32), -1)
            x_row = (xh * gain1 + shift1).astype(BF16)
            x_v[r, rk, :] = x_row
            project(s_ref, i, x_row, m_v[r, 0:1, rk], wpt_v[1], c)
            return carry2

        each_row(row)
        pack_ab(s_ref, c, abr, ri, rk)
        send_ab(2, q, ab1)
        return carry

    lax.fori_loop(0, nq, step2, 0)
    drain(t_c, osem.at[1])
    drain_all(nq, t_part, snd(1))
    drain_all(nq, ab_part, snd(2))
    load_g.wait()
    drain_all(nq, ab_part, rcv(2))

    def product1(j):
        ts[j, :, :] = dot(ab1[0, j], ab1[1, j], 0, 0).astype(BF16)

    exchange_t(3, product1)

    def step3(q, carry):
        ri, rk, i0 = block(q, cols)
        drain(t_part, rcv(3)(q))

        def write_t(sl, val):
            t_c[:, sl, :] = val

        unpack(lambda sl: tr[sl, ri, rk], c, write_t)

        @pl.when(q > 0)
        def _():
            drain(zo_c, osem.at[2])

        def row(i, carry2):
            r = i0 + i
            th, rstd = norm(t_c[i].astype(F32), 0)
            y = (th * gq_v[1, 0] + gq_v[1, 1]).astype(BF16)
            upd = dot(y, wo_ref[1], 0, 0)
            gate = jax.nn.sigmoid(dot(x_v[r, rk, :], wg_ref[1], 1, 0))
            zo_c[i] = (z_v[r, rk, :].astype(F32) + gate * upd).astype(BF16)
            finish_back(i, r, rk, g_v[r, rk, :].astype(F32), th, rstd, y, upd, gate, gq_v[1, 0], wo_ref[1], dg_v, s_ref, gwo, glq, 1)
            return carry2

        each_row(row)
        pltpu.make_async_copy(zo_c, zo_hbm.at[ri, rk, :], osem.at[2]).start()

        def write(sl, val):
            tr[sl, ri, rk] = val

        pack(s_ref, 0, c, write)
        send_dt(4, q)
        return carry

    lax.fori_loop(0, nq, step3, 0)
    drain(zo_c, osem.at[2])
    drain_all(nq, t_part, snd(3))
    drain_all(nq, dt_part, snd(4))
    drain_all(nq, dt_part, rcv(4))
    exchange_dab(5, True, ab1)

    def step4(q, carry):
        ri, rk, i0 = block(q, cols)
        load_t = pltpu.make_async_copy(t0_hbm.at[ri, :, rk], t_c, isem.at[2])
        load_x = pltpu.make_async_copy(x0_hbm.at[ri, rk, :], xp_c, isem.at[3])
        load_t.start()
        load_x.start()
        drain(dab_part, rcv(5)(q))
        unpack_dab(abr, dab_t, c, ri, rk)
        load_t.wait()
        load_x.wait()

        def row(i, carry2):
            r = i0 + i
            dn = project_back(1, i, r, rk, dab_t, m_v, x_v, z_v, dg_v, g_v, gain1, wpt_v, wp_ref, wg_ref, gwp, gwg, glp, c)
            g_v[r, rk, :] = dn
            th, rstd = norm(t_c[i].astype(F32), 0)
            y = (th * gq_v[0, 0] + gq_v[0, 1]).astype(BF16)
            upd = dot(y, wo_ref[0], 0, 0)
            gate = jax.nn.sigmoid(dot(xp_c[i], wg_ref[0], 1, 0))
            finish_back(i, r, rk, dn.astype(F32), th, rstd, y, upd, gate, gq_v[0, 0], wo_ref[0], dg_v, s_ref, gwo, glq, 0)
            return carry2

        each_row(row)

        def write(sl, val):
            tr[sl, ri, rk] = val

        pack(s_ref, 0, c, write)
        send_dt(6, q)
        return carry

    lax.fori_loop(0, nq, step4, 0)
    reload_z = pltpu.make_async_copy(z_hbm, z_v, isem.at[0])
    reload_x = pltpu.make_async_copy(x0_hbm, x_v, isem.at[1])
    reload_z.start()
    reload_x.start()
    small = [jnp.sum(glp[1, h], axis=0, keepdims=True) for h in range(2)]
    small += [jnp.sum(glq[u, h].T, axis=0, keepdims=True) for u in (1, 0) for h in range(2)]
    small = jnp.concatenate(small + [jnp.zeros((2, c), F32)], axis=0)
    e1, e2, e3, e4 = we, we + wc, we + 2 * wc, we + 3 * wc

    def fill(p, carry):
        z, k = p // 2, lax.rem(p, 2)
        cut = pl.ds(pl.multiple_of(p * wc, 8), wc)
        early[z, k, 0:e1, :] = gwp[1, pl.ds(pl.multiple_of(p * we, 8), we), :]
        early[z, k, e1:e2, :] = gwg[1, cut, :]
        early[z, k, e2:e3, :] = gwo[1, cut, :]
        early[z, k, e3:e4, :] = gwo[0, cut, :]
        early[z, k, e4:e4 + 8, :] = small
        return carry

    lax.fori_loop(0, n, fill, 0)
    to_pair(n, me, early.at[:, 1 - core], pair_e, gss.at[0], grs.at[0])
    drain_all(nq, dab_part, snd(5))
    drain_all(nq, dt_part, snd(6))
    drain_all(nq, dt_part, rcv(6))
    exchange_dab(7, False, ab0)
    drain(pair_e, grs.at[0])
    pair_sum(core, early, pair_e, comb_e)
    gath_e[chip] = comb_e[chip]
    to_chips(n, me, lambda o: comb_e.at[o], lambda d: gath_e.at[d], gss.at[1], grs.at[1])
    reload_z.wait()
    reload_x.wait()

    def step5(q, carry):
        ri, rk, i0 = block(q, cols)
        drain(dab_part, rcv(7)(q))
        unpack_dab(abr, dab_t, c, ri, rk)

        def row(i, carry2):
            r = i0 + i
            g_v[r, rk, :] = project_back(0, i, r, rk, dab_t, m_v, x_v, z_v, dg_v, g_v, gain0, wpt_v, wp_ref, wg_ref, gwp, gwg, glp, c)
            return carry2

        each_row(row)
        pltpu.make_async_copy(g_v.at[ri, rk, :], dz_hbm.at[ri, rk, :], osem.at[3]).start()
        return carry

    lax.fori_loop(0, nq, step5, 0)
    tail = jnp.concatenate([jnp.sum(glp[0, h], axis=0, keepdims=True) for h in range(2)] + [jnp.zeros((6, c), F32)], axis=0)

    def fill_late(p, carry):
        z, k = p // 2, lax.rem(p, 2)
        late[z, k, 0:e1, :] = gwp[0, pl.ds(pl.multiple_of(p * we, 8), we), :]
        late[z, k, e1:e2, :] = gwg[0, pl.ds(pl.multiple_of(p * wc, 8), wc), :]
        late[z, k, e2:e2 + 8, :] = tail
        return carry

    lax.fori_loop(0, n, fill_late, 0)
    to_pair(n, me, late.at[:, 1 - core], pair_l, gss.at[2], grs.at[2])
    drain(gath_e.at[pl.ds(0, n // 2 - 1)], grs.at[1])
    sum_e = add_parts(gath_e)
    drain(pair_l, grs.at[2])
    pair_sum(core, late, pair_l, comb_l)
    gath_l[chip] = comb_l[chip]
    to_chips(n, me, lambda o: comb_l.at[o], lambda d: gath_l.at[d], gss.at[3], grs.at[3])
    drain(gath_l.at[pl.ds(0, n // 2 - 1)], grs.at[3])
    sum_l = add_parts(gath_l)
    mine[...] = jnp.concatenate([sum_e[0:e1], sum_l[0:e1], sum_e[e1:e4], sum_l[e1:e2]], axis=0).astype(BF16)
    to_chips(n, me, lambda o: mine, lambda d: all_v.at[core, d], gss.at[4], grs.at[4])
    all_v[core, chip] = mine[...]
    small_ref[0:8, :] = sum_e[e4:e4 + 8]
    small_ref[8:16, :] = sum_l[e2:e2 + 8]
    drain(dz_hbm, osem.at[3])
    drain_all(nq, dab_part, snd(7))
    drain(pair_e, gss.at[0])
    drain(gath_e.at[pl.ds(0, n // 2 - 1)], gss.at[1])
    drain(pair_l, gss.at[2])
    drain(gath_l.at[pl.ds(0, n // 2 - 1)], gss.at[3])
    others = all_v.at[0, pl.ds(0, n // 2 - 1)]
    drain(others, gss.at[4])
    drain(others, grs.at[4])
    to_pair(n, me, all_v.at[core], all_v.at[core], gss.at[5], grs.at[5])
    drain(all_v.at[core], gss.at[5])
    drain(all_v.at[1 - core], grs.at[5])
    grads_ref[...] = all_v[...]


def solution(mesh):
    row_spec = P(('data', AXIS), None, None)
    mask_spec = P(('data', AXIS), None)
    grad_spec = P('data', None, None)
    n = mesh.shape[AXIS]

    def device_step(z0, mask, g, ln_pair, w_proj, w_gate, ln_chan, w_out):
        rows, cols, c = z0.shape
        cl = c // n
        nq = (rows // RB) * (cols // KB)
        we, wc = 4 * c // n, c // n
        er, lr, gr = we + 3 * wc + 8, we + wc + 8, 2 * we + 4 * wc
        half = n // 2
        vm = pltpu.VMEM
        dma = pltpu.SemaphoreType.DMA
        row_t = jax.ShapeDtypeStruct((rows, cols, c), BF16)
        row_v = vm((rows, cols, c), BF16)
        chan_v = vm((cl, cols, cols), BF16)
        scratch = [vm((2, cl, cols, cols), BF16)] * 2 + [vm((2, c, rows, cols), BF16), chan_v, vm((c, rows, cols), BF16), chan_v] + [row_v] * 4
        scratch += [vm((RB, 2 * c, KB), F32), vm((RB, 2 * c, KB), BF16), vm((RB, c, KB), BF16), vm((RB, KB, c), BF16), vm((RB, KB, c), BF16)]
        scratch += [vm((2, 4 * c, c), BF16), vm((2, 2, c, KB), F32), vm((rows, 1, cols), F32)]
        scratch += [vm((2, 4 * c, c), F32), vm((2, c, c), F32), vm((2, c, c), F32), vm((2, 2, 8, c), F32), vm((2, 2, c, 128), F32)]
        for k in (er, lr):
            scratch += [vm((half, 2, k, c), F32)] + [vm((half, k, c), F32)] * 3
        scratch += [vm((gr, c), BF16), vm((2, half, gr, c), BF16)]
        scratch += [dma((8, 2, nq)), dma((4,)), dma((4,)), dma((6,)), dma((6,))]
        z2, dz, _, _, grads, small = pl.pallas_call(
            functools.partial(whole_kernel, n),
            out_shape=(row_t, row_t, row_t, jax.ShapeDtypeStruct((rows, c, cols), BF16), jax.ShapeDtypeStruct((2, half, gr, c), BF16), jax.ShapeDtypeStruct((16, c), F32)),
            in_specs=[ANY, VM, ANY] + [VM] * 5,
            out_specs=(ANY, ANY, ANY, ANY, VM, VM),
            scratch_shapes=scratch,
            compiler_params=pltpu.CompilerParams(collective_id=1, has_side_effects=True, vmem_limit_bytes=67043328),
            name='whole',
        )(z0, mask, g, ln_pair, w_proj, w_gate, ln_chan, w_out)

        def rows_of(start, count):
            return jnp.swapaxes(grads[:, :, start:start + count], 0, 1).reshape(n * count, c)

        base = 2 * we
        d_wp = jnp.stack([rows_of(we, we).T, rows_of(0, we).T])
        d_wg = jnp.stack([rows_of(base + 3 * wc, wc), rows_of(base, wc)])
        d_wo = jnp.stack([rows_of(base + 2 * wc, wc), rows_of(base + wc, wc)])
        small = small.astype(BF16)
        d_lp = jnp.stack([small[8:10], small[0:2]])
        d_lq = jnp.stack([small[4:6], small[2:4]])
        return z2, dz, d_lp, d_wp, d_wg, d_lq, d_wo

    full = P()
    return jax.shard_map(device_step, mesh=mesh, in_specs=(row_spec, mask_spec, row_spec, full, full, full, full, full), out_specs=(row_spec, row_spec, grad_spec, grad_spec, grad_spec, grad_spec, grad_spec), check_vma=False)
```

time: 1720 us -> 1170 us (0.68)
  Pallas kernels: 0 us -> 1160 us
  blocking collectives: 646 us -> 0 us
  waiting for transfers between devices: 462 us -> 0 us
  other arithmetic: 221 us -> 1.97 us
  local copies, waits for them, and re-layouts: 186 us -> 9.54 us
  matrix products: 175 us -> 0 us
  starting transfers between devices: 20.4 us -> 0 us
    pallas_call x0 -> x1, Pallas kernels: none -> 1160 us  [device_step(): pl.pallas_call(functools.partial(whole_kernel, n), out_shape=(row_t, row_...]
    all_to_all x4 -> x0, blocking collectives: 594 us -> none  [to_channels(): lax.all_to_all(row_blocks, GROUP_AXIS, chan_dim, chan_dim + 1, tiled=True)]
    all_to_all x4 -> x0, waiting for transfers between devices: 462 us -> none  [to_rows(): lax.all_to_all(chan_blocks, GROUP_AXIS, chan_dim + 1, chan_dim, tiled=True)]
    dot_general x24 -> x0, matrix products: 175 us -> none  [the longest x2 26.6 us: update_forward(): jnp.einsum('ijd,de->eij', x_norm, w_proj, preferred_element_type=jnp.floa...]
    another operation x17 -> x3, other arithmetic: 98.6 us -> 1.27 us  [the longest x1 0.67 us: device_step(): d_wg = jnp.stack([rows_of(base + 3 * wc, wc), rows_of(base, wc)])]
    convert_element_type x12 -> x1, other arithmetic: 66.7 us -> 0.7 us  [device_step(): small = small.astype(BF16)]
    convert_element_type x10 -> x0, local copies, waits for them, and re-layouts: 58.3 us -> none  [the longest x4 32.9 us: update_forward(): t_rows.astype(jnp.float32)]
    reduce_sum x13 -> x0, other arithmetic: 55.4 us -> none  [the longest x6 38.5 us: layer_norm(): return centered * lax.rsqrt(variance + LN_EPS) * gain_vec + shift_vec]
  transfers between devices with their start and end apart: 4 -> 0, of which waited for: 4 -> 0; matrix products, arithmetic and copies ran while one was open for 6% -> 0% of each run, Pallas kernels for 0% -> 0%
where the time goes in v3:
time: 1170 us
  Pallas kernels  1160 us (99%)
    pallas_call x1, Pallas kernels, device_step(): pl.pallas_call(functools.partial(whole_kernel, n), out_shape=(row_t, row_...  1160 us

profile of v3, /device:TPU:23, one launch (start us, length us, event | category | flops | bytes accessed | tf_op | source)
XLA Modules:
  0.0 1167.8 jit_solution(1117420711494547710)
XLA Ops:
  0.6 1155.6 %whole.1 = (bf16[32,512,128]{2,1,0:T(8,128)(2,1)}, bf16[32,512,128]{2,1,0:T(8,128)(2,1)}, bf16[32,512,128]{2,1,0:T(8,128)(2,1)}, bf16[32,128,512]{2,1,0:T(8,128)...) custom-call(bf16[32,512,128]{2,1,0:T(8,128)(2,1)} %z_hbm.1, s32[32,512]{1,0:T(8,128)} %m_ref.1, ...), custom_call_target="tpu_custom_call" | custom-call | tf_op jit(solution)/shard_map/whole/pallas_call | solution.py:609
  1156.2 0.7 convert_element_type.3
  1156.9 0.6 pad_maximum_fusion.3
  1157.5 0.8 slice_bitcast_fusion.3
  1158.3 1.0 slice_bitcast_fusion.1
  1159.4 0.7 pad_maximum_fusion.1
  1160.1 0.9 copy.21
  1161.0 0.0 copy-start
  1161.0 4.8 copy.24
  1165.8 0.0 copy-done
  1165.8 2.0 copy.25
  (8 shorter events, 0.1 us)
Async XLA Ops:
  1161.0 4.8 copy-start

commit v4 on v3

--- a/solution.py
+++ b/solution.py
@@ -118,13 +118,37 @@
 
 
 def each_row(row):
-    lax.fori_loop(0, RB, row, 0, unroll=UNROLL)
+    def pair(k, carry):
+        return row(2 * k, carry)
+
+    lax.fori_loop(0, RB // 2, pair, 0, unroll=UNROLL)
+
+
+def get_rows(ref, r, rk):
+    return ref[pl.ds(r, 2), rk, :].reshape(2 * KB, ref.shape[2])
+
+
+def put_rows(ref, r, rk, val):
+    ref[pl.ds(r, 2), rk, :] = val.reshape(2, KB, val.shape[1])
+
+
+def get_lanes(ref, i, lo, hi):
+    return jnp.concatenate([ref[i, lo:hi, :].astype(F32), ref[i + 1, lo:hi, :].astype(F32)], axis=1)
+
+
+def put_lanes(ref, i, lo, hi, val):
+    ref[i, lo:hi, :] = val[:, :KB]
+    ref[i + 1, lo:hi, :] = val[:, KB:]
+
+
+def get_mask(m_v, r, rk):
+    return jnp.concatenate([m_v[r, 0:1, rk], m_v[r + 1, 0:1, rk]], axis=1)
 
 
 def project(s_ref, i, x_row, m_row, w_t, c):
     p = dot(w_t, x_row, 1, 1)
-    s_ref[i, 0:c, :] = m_row * jax.nn.sigmoid(p[c:2 * c]) * p[0:c]
-    s_ref[i, c:2 * c, :] = m_row * jax.nn.sigmoid(p[3 * c:]) * p[2 * c:3 * c]
+    put_lanes(s_ref, i, 0, c, m_row * jax.nn.sigmoid(p[c:2 * c]) * p[0:c])
+    put_lanes(s_ref, i, c, 2 * c, m_row * jax.nn.sigmoid(p[3 * c:]) * p[2 * c:3 * c])
 
 
 def fold_rows(v):
@@ -155,7 +179,7 @@
 def finish_back(i, r, rk, dn, th, rstd, y, upd, gate, gain, w_out, dg_v, s_ref, gwo, glq, u):
     d_gate = dn * upd * gate * (1.0 - gate)
     d_upd = (dn * gate).astype(BF16)
-    dg_v[r, rk, :] = d_gate.astype(BF16)
+    put_rows(dg_v, r, rk, d_gate.astype(BF16))
     gwo[u] += dot(y, d_upd, 1, 0)
     dy = dot(w_out, d_upd, 1, 1).astype(BF16).astype(F32)
     glq[u, 0] += fold_lanes(dy * th)
@@ -163,34 +187,34 @@
     dyg = dy * gain
     m1 = jnp.mean(dyg, axis=0, keepdims=True)
     m2 = jnp.mean(dyg * th, axis=0, keepdims=True)
-    s_ref[i, 0:dy.shape[0], :] = rstd * (dyg - m1 - th * m2)
+    put_lanes(s_ref, i, 0, dy.shape[0], rstd * (dyg - m1 - th * m2))
 
 
 def project_back(u, i, r, rk, dab_t, m_v, x_v, z_v, dg_v, dn_v, gain, wpt_v, wp_ref, wg_ref, gwp, gwg, glp, c):
-    x_row = x_v[r, rk, :]
-    m_row = m_v[r, 0:1, rk]
+    x_row = get_rows(x_v, r, rk)
+    m_row = get_mask(m_v, r, rk)
     p = dot(wpt_v[u], x_row, 1, 1)
     parts = []
     for h in range(2):
-        d_val = dab_t[i, h * c:(h + 1) * c, :].astype(F32) * m_row
+        d_val = get_lanes(dab_t, i, h * c, (h + 1) * c) * m_row
         lin = p[2 * h * c:(2 * h + 1) * c]
         sig = jax.nn.sigmoid(p[(2 * h + 1) * c:(2 * h + 2) * c])
         d_lin = d_val * sig
         parts.append(d_lin.astype(BF16))
         parts.append((d_lin * lin * (1.0 - sig)).astype(BF16))
     d_proj = jnp.concatenate(parts, axis=0)
-    d_gate = dg_v[r, rk, :]
+    d_gate = get_rows(dg_v, r, rk)
     gwp[u] += dot(d_proj, x_row, 1, 0)
     gwg[u] += dot(x_row, d_gate, 0, 0)
     dxt = dot(wp_ref[u], d_proj, 1, 0) + dot(wg_ref[u], d_gate, 1, 1)
     dx = dxt.T.astype(BF16).astype(F32)
-    xh, rstd = norm(z_v[r, rk, :].astype(F32), -1)
+    xh, rstd = norm(get_rows(z_v, r, rk).astype(F32), -1)
     glp[u, 0] += fold_rows(dx * xh)
     glp[u, 1] += fold_rows(dx)
     dxg = dx * gain
     m1 = jnp.mean(dxg, axis=-1, keepdims=True)
     m2 = jnp.mean(dxg * xh, axis=-1, keepdims=True)
-    return (dn_v[r, rk, :].astype(F32) + rstd * (dxg - m1 - xh * m2)).astype(BF16)
+    return (get_rows(dn_v, r, rk).astype(F32) + rstd * (dxg - m1 - xh * m2)).astype(BF16)
 
 
 def to_pair(n, me, src, dst, ssem, rsem):
@@ -241,14 +265,16 @@
     me = greet(n)
     core, chip = lax.rem(me, 2), me // 2
 
-    def snd(k):
-        return lambda q: sems.at[k, 0, q]
-
-    def rcv(k):
-        return lambda q: sems.at[k, 1, q]
-
-    ab_part = ab0.at[:, :, pl.ds(0, RB * (n - 1)), pl.ds(0, KB)]
-    dt_part = dt.at[:, pl.ds(0, RB * (n - 1)), pl.ds(0, KB)]
+    def snd(k, h=0):
+        return lambda q: sems.at[k, h, 0, q]
+
+    def rcv(k, h=0):
+        return lambda q: sems.at[k, h, 1, q]
+
+    hc = cl // 2
+
+    ab_part = ab0.at[:, pl.ds(0, cl // 2), pl.ds(0, RB * (n - 1)), pl.ds(0, KB)]
+    dt_part = dt.at[pl.ds(0, cl // 2), pl.ds(0, RB * (n - 1)), pl.ds(0, KB)]
     t_part = tr.at[pl.ds(0, c - cl), pl.ds(0, RB), pl.ds(0, KB)]
     dab_part = abr.at[:, pl.ds(0, c - cl), pl.ds(0, RB), pl.ds(0, KB)]
 
@@ -258,7 +284,8 @@
         def at(dev):
             return pl.ds(pl.multiple_of(dev * rows + i0, RB), RB)
 
-        scatter(n, me, lambda p: abr.at[:, pl.ds(p * cl, cl), ri, rk], lambda d: dest.at[:, :, at(d), rk], snd(k)(q), rcv(k)(q))
+        for e in range(2):
+            scatter(n, me, lambda p, e=e: abr.at[:, pl.ds(p * cl + e * hc, hc), ri, rk], lambda d, e=e: dest.at[:, pl.ds(e * hc, hc), at(d), rk], snd(k, e)(q), rcv(k, e)(q))
 
         def own(j, carry):
             for h in range(2):
@@ -273,7 +300,8 @@
         def at(dev):
             return pl.ds(pl.multiple_of(dev * rows + i0, RB), RB)
 
-        scatter(n, me, lambda p: tr.at[pl.ds(p * cl, cl), ri, rk], lambda d: dt.at[:, at(d), rk], snd(k)(q), rcv(k)(q))
+        for e in range(2):
+            scatter(n, me, lambda p, e=e: tr.at[pl.ds(p * cl + e * hc, hc), ri, rk], lambda d, e=e: dt.at[pl.ds(e * hc, hc), at(d), rk], snd(k, e)(q), rcv(k, e)(q))
 
         def own(j, carry):
             dt[j, at(me), rk] = tr[me * cl + j, ri, rk]
@@ -281,8 +309,13 @@
 
         lax.fori_loop(0, cl, own, 0)
 
-    def exchange(product, send):
+    def exchange(product, send, arrived):
         def one(j, carry):
+            for e in range(2):
+                @pl.when(j == e * hc)
+                def _(e=e):
+                    arrived(e)
+
             product(j)
             send(j, 1, 0)
             return carry
@@ -295,12 +328,12 @@
 
         lax.fori_loop(1, nq, rest, 0)
 
-    def exchange_t(k, product):
+    def exchange_t(k, product, arrived):
         def send(j, count, q):
             ri, rk, i0 = block(q, cols)
             scatter(n, me, lambda p: ts.at[pl.ds(j, count), pl.ds(pl.multiple_of(p * rows + i0, RB), RB), rk], lambda d: tr.at[pl.ds(d * cl + j, count), ri, rk], snd(k)(q), rcv(k)(q))
 
-        exchange(product, send)
+        exchange(product, send, arrived)
 
         def own(j, carry):
             tr[me * cl + j, :, :] = ts[j, pl.ds(pl.multiple_of(me * rows, RB), rows), :]
@@ -308,7 +341,7 @@
 
         lax.fori_loop(0, cl, own, 0)
 
-    def exchange_dab(k, incoming, ab):
+    def exchange_dab(k, incoming, ab, arrived):
         def product(j):
             left, right, d_t = ab[0, j], ab[1, j], dt[j]
             if incoming:
@@ -324,7 +357,7 @@
             ri, rk, i0 = block(q, cols)
             scatter(n, me, lambda p: ab.at[:, pl.ds(j, count), pl.ds(pl.multiple_of(p * rows + i0, RB), RB), rk], lambda d: abr.at[:, pl.ds(d * cl + j, count), ri, rk], snd(k)(q), rcv(k)(q))
 
-        exchange(product, send)
+        exchange(product, send, arrived)
 
         def own(j, carry):
             for h in range(2):
@@ -344,10 +377,10 @@
 
         def row(i, carry2):
             r = i0 + i
-            xh, _ = norm(z_v[r, rk, :].astype(F32), -1)
+            xh, _ = norm(get_rows(z_v, r, rk).astype(F32), -1)
             x_row = (xh * gain0 + shift0).astype(BF16)
-            x_v[r, rk, :] = x_row
-            project(s_ref, i, x_row, m_v[r, 0:1, rk], wpt_v[0], c)
+            put_rows(x_v, r, rk, x_row)
+            project(s_ref, i, x_row, get_mask(m_v, r, rk), wpt_v[0], c)
             return carry2
 
         each_row(row)
@@ -368,13 +401,13 @@
     for ref in (gwp, gwg, gwo, glp, glq):
         ref[...] = jnp.zeros_like(ref)
     drain(x_v, osem.at[0])
-    drain_all(nq, ab_part, snd(0))
-    drain_all(nq, ab_part, rcv(0))
 
     def product0(j):
         ts[j, :, :] = dot(ab0[0, j], ab0[1, j], 1, 1).astype(BF16)
 
-    exchange_t(1, product0)
+    exchange_t(1, product0, lambda e: drain_all(nq, ab_part, rcv(0, e)))
+    for e in range(2):
+        drain_all(nq, ab_part, snd(0, e))
 
     def step2(q, carry):
         ri, rk, i0 = block(q, cols)
@@ -393,16 +426,16 @@
 
         def row(i, carry2):
             r = i0 + i
-            th, _ = norm(t_c[i].astype(F32), 0)
+            th, _ = norm(get_lanes(t_c, i, 0, c), 0)
             y = (th * gq_v[0, 0] + gq_v[0, 1]).astype(BF16)
             upd = dot(y, wo_ref[0], 0, 0)
-            gate = jax.nn.sigmoid(dot(x_v[r, rk, :], wg_ref[0], 1, 0))
-            z_new = (z_v[r, rk, :].astype(F32) + gate * upd).astype(BF16)
-            z_v[r, rk, :] = z_new
+            gate = jax.nn.sigmoid(dot(get_rows(x_v, r, rk), wg_ref[0], 1, 0))
+            z_new = (get_rows(z_v, r, rk).astype(F32) + gate * upd).astype(BF16)
+            put_rows(z_v, r, rk, z_new)
             xh, _ = norm(z_new.astype(F32), -1)
             x_row = (xh * gain1 + shift1).astype(BF16)
-            x_v[r, rk, :] = x_row
-            project(s_ref, i, x_row, m_v[r, 0:1, rk], wpt_v[1], c)
+            put_rows(x_v, r, rk, x_row)
+            project(s_ref, i, x_row, get_mask(m_v, r, rk), wpt_v[1], c)
             return carry2
 
         each_row(row)
@@ -413,14 +446,14 @@
     lax.fori_loop(0, nq, step2, 0)
     drain(t_c, osem.at[1])
     drain_all(nq, t_part, snd(1))
-    drain_all(nq, ab_part, snd(2))
     load_g.wait()
-    drain_all(nq, ab_part, rcv(2))
 
     def product1(j):
         ts[j, :, :] = dot(ab1[0, j], ab1[1, j], 0, 0).astype(BF16)
 
-    exchange_t(3, product1)
+    exchange_t(3, product1, lambda e: drain_all(nq, ab_part, rcv(2, e)))
+    for e in range(2):
+        drain_all(nq, ab_part, snd(2, e))
 
     def step3(q, carry):
         ri, rk, i0 = block(q, cols)
@@ -437,12 +470,12 @@
 
         def row(i, carry2):
             r = i0 + i
-            th, rstd = norm(t_c[i].astype(F32), 0)
+            th, rstd = norm(get_lanes(t_c, i, 0, c), 0)
             y = (th * gq_v[1, 0] + gq_v[1, 1]).astype(BF16)
             upd = dot(y, wo_ref[1], 0, 0)
-            gate = jax.nn.sigmoid(dot(x_v[r, rk, :], wg_ref[1], 1, 0))
-            zo_c[i] = (z_v[r, rk, :].astype(F32) + gate * upd).astype(BF16)
-            finish_back(i, r, rk, g_v[r, rk, :].astype(F32), th, rstd, y, upd, gate, gq_v[1, 0], wo_ref[1], dg_v, s_ref, gwo, glq, 1)
+            gate = jax.nn.sigmoid(dot(get_rows(x_v, r, rk), wg_ref[1], 1, 0))
+            put_rows(zo_c, i, slice(None), (get_rows(z_v, r, rk).astype(F32) + gate * upd).astype(BF16))
+            finish_back(i, r, rk, get_rows(g_v, r, rk).astype(F32), th, rstd, y, upd, gate, gq_v[1, 0], wo_ref[1], dg_v, s_ref, gwo, glq, 1)
             return carry2
 
         each_row(row)
@@ -457,10 +490,10 @@
 
     lax.fori_loop(0, nq, step3, 0)
     drain(zo_c, osem.at[2])
+    exchange_dab(5, True, ab1, lambda e: drain_all(nq, dt_part, rcv(4, e)))
     drain_all(nq, t_part, snd(3))
-    drain_all(nq, dt_part, snd(4))
-    drain_all(nq, dt_part, rcv(4))
-    exchange_dab(5, True, ab1)
+    for e in range(2):
+        drain_all(nq, dt_part, snd(4, e))
 
     def step4(q, carry):
         ri, rk, i0 = block(q, cols)
@@ -476,11 +509,11 @@
         def row(i, carry2):
             r = i0 + i
             dn = project_back(1, i, r, rk, dab_t, m_v, x_v, z_v, dg_v, g_v, gain1, wpt_v, wp_ref, wg_ref, gwp, gwg, glp, c)
-            g_v[r, rk, :] = dn
-            th, rstd = norm(t_c[i].astype(F32), 0)
+            put_rows(g_v, r, rk, dn)
+            th, rstd = norm(get_lanes(t_c, i, 0, c), 0)
             y = (th * gq_v[0, 0] + gq_v[0, 1]).astype(BF16)
             upd = dot(y, wo_ref[0], 0, 0)
-            gate = jax.nn.sigmoid(dot(xp_c[i], wg_ref[0], 1, 0))
+            gate = jax.nn.sigmoid(dot(get_rows(xp_c, i, slice(None)), wg_ref[0], 1, 0))
             finish_back(i, r, rk, dn.astype(F32), th, rstd, y, upd, gate, gq_v[0, 0], wo_ref[0], dg_v, s_ref, gwo, glq, 0)
             return carry2
 
@@ -515,10 +548,10 @@
 
     lax.fori_loop(0, n, fill, 0)
     to_pair(n, me, early.at[:, 1 - core], pair_e, gss.at[0], grs.at[0])
+    exchange_dab(7, False, ab0, lambda e: drain_all(nq, dt_part, rcv(6, e)))
     drain_all(nq, dab_part, snd(5))
-    drain_all(nq, dt_part, snd(6))
-    drain_all(nq, dt_part, rcv(6))
-    exchange_dab(7, False, ab0)
+    for e in range(2):
+        drain_all(nq, dt_part, snd(6, e))
     drain(pair_e, grs.at[0])
     pair_sum(core, early, pair_e, comb_e)
     gath_e[chip] = comb_e[chip]
@@ -533,7 +566,8 @@
 
         def row(i, carry2):
             r = i0 + i
-            g_v[r, rk, :] = project_back(0, i, r, rk, dab_t, m_v, x_v, z_v, dg_v, g_v, gain0, wpt_v, wp_ref, wg_ref, gwp, gwg, glp, c)
+            dn = project_back(0, i, r, rk, dab_t, m_v, x_v, z_v, dg_v, g_v, gain0, wpt_v, wp_ref, wg_ref, gwp, gwg, glp, c)
+            put_rows(g_v, r, rk, dn)
             return carry2
 
         each_row(row)
@@ -600,12 +634,12 @@
         chan_v = vm((cl, cols, cols), BF16)
         scratch = [vm((2, cl, cols, cols), BF16)] * 2 + [vm((2, c, rows, cols), BF16), chan_v, vm((c, rows, cols), BF16), chan_v] + [row_v] * 4
         scratch += [vm((RB, 2 * c, KB), F32), vm((RB, 2 * c, KB), BF16), vm((RB, c, KB), BF16), vm((RB, KB, c), BF16), vm((RB, KB, c), BF16)]
-        scratch += [vm((2, 4 * c, c), BF16), vm((2, 2, c, KB), F32), vm((rows, 1, cols), F32)]
+        scratch += [vm((2, 4 * c, c), BF16), vm((2, 2, c, 2 * KB), F32), vm((rows, 1, cols), F32)]
         scratch += [vm((2, 4 * c, c), F32), vm((2, c, c), F32), vm((2, c, c), F32), vm((2, 2, 8, c), F32), vm((2, 2, c, 128), F32)]
         for k in (er, lr):
             scratch += [vm((half, 2, k, c), F32)] + [vm((half, k, c), F32)] * 3
         scratch += [vm((gr, c), BF16), vm((2, half, gr, c), BF16)]
-        scratch += [dma((8, 2, nq)), dma((4,)), dma((4,)), dma((6,)), dma((6,))]
+        scratch += [dma((8, 2, 2, nq)), dma((4,)), dma((4,)), dma((6,)), dma((6,))]
         z2, dz, _, _, grads, small = pl.pallas_call(
             functools.partial(whole_kernel, n),
             out_shape=(row_t, row_t, row_t, jax.ShapeDtypeStruct((rows, c, cols), BF16), jax.ShapeDtypeStruct((2, half, gr, c), BF16), jax.ShapeDtypeStruct((16, c), F32)),

time: 1170 us -> 1160 us (level)
  Pallas kernels: 1160 us -> 1140 us
    pallas_call x1, Pallas kernels: 1160 us -> 1140 us  [device_step(): pl.pallas_call(functools.partial(whole_kernel, n), out_shape=(row_t, row_...]
where the time goes in v4:
time: 1160 us; the launch traced here: 1150 us
  Pallas kernels  1140 us (98%)
    pallas_call x1, Pallas kernels, device_step(): pl.pallas_call(functools.partial(whole_kernel, n), out_shape=(row_t, row_...  1140 us

profile of v4, /device:TPU:23, one launch (start us, length us, event | category | flops | bytes accessed | tf_op | source)
XLA Modules:
  0.0 1149.3 jit_solution(7468161995433949520)
XLA Ops:
  0.6 1137.1 %whole.1 = (bf16[32,512,128]{2,1,0:T(8,128)(2,1)}, bf16[32,512,128]{2,1,0:T(8,128)(2,1)}, bf16[32,512,128]{2,1,0:T(8,128)(2,1)}, bf16[32,128,512]{2,1,0:T(8,128)...) custom-call(bf16[32,512,128]{2,1,0:T(8,128)(2,1)} %z_hbm.1, s32[32,512]{1,0:T(8,128)} %m_ref.1, ...), custom_call_target="tpu_custom_call" | custom-call | tf_op jit(solution)/shard_map/whole/pallas_call | solution.py:643
  1137.7 0.7 convert_element_type.3
  1138.5 0.6 pad_maximum_fusion.3
  1139.0 0.8 slice_bitcast_fusion.3
  1139.8 1.0 slice_bitcast_fusion.1
  1140.9 0.7 pad_maximum_fusion.1
  1141.6 0.9 copy.21
  1142.5 0.0 copy-start
  1142.5 4.8 copy.24
  1147.3 0.0 copy-done
  1147.3 2.0 copy.25
  (8 shorter events, 0.1 us)
Async XLA Ops:
  1142.5 4.8 copy-start

commit v5 on v4

--- a/solution.py
+++ b/solution.py
@@ -309,18 +309,23 @@
 
         lax.fori_loop(0, cl, own, 0)
 
-    def exchange(product, send, arrived):
+    def exchange(product, send, arrived, batch):
         def one(j, carry):
+            product(j)
+            return carry
+
+        def some(b, carry):
+            j0 = b * batch
             for e in range(2):
-                @pl.when(j == e * hc)
+                @pl.when(j0 == e * hc)
                 def _(e=e):
                     arrived(e)
 
-            product(j)
-            send(j, 1, 0)
+            lax.fori_loop(j0, j0 + batch, one, 0)
+            send(j0, batch, 0)
             return carry
 
-        lax.fori_loop(0, cl, one, 0)
+        lax.fori_loop(0, cl // batch, some, 0)
 
         def rest(q, carry):
             send(0, cl, q)
@@ -333,7 +338,7 @@
             ri, rk, i0 = block(q, cols)
             scatter(n, me, lambda p: ts.at[pl.ds(j, count), pl.ds(pl.multiple_of(p * rows + i0, RB), RB), rk], lambda d: tr.at[pl.ds(d * cl + j, count), ri, rk], snd(k)(q), rcv(k)(q))
 
-        exchange(product, send, arrived)
+        exchange(product, send, arrived, hc)
 
         def own(j, carry):
             tr[me * cl + j, :, :] = ts[j, pl.ds(pl.multiple_of(me * rows, RB), rows), :]
@@ -357,7 +362,7 @@
             ri, rk, i0 = block(q, cols)
             scatter(n, me, lambda p: ab.at[:, pl.ds(j, count), pl.ds(pl.multiple_of(p * rows + i0, RB), RB), rk], lambda d: abr.at[:, pl.ds(d * cl + j, count), ri, rk], snd(k)(q), rcv(k)(q))
 
-        exchange(product, send, arrived)
+        exchange(product, send, arrived, hc // 2)
 
         def own(j, carry):
             for h in range(2):

time: 1160 us -> 1150 us (level); the launches traced: 1150 us -> 1150 us
  no operation moved by 1% of the time
where the time goes in v5:
time: 1150 us
  Pallas kernels  1140 us (99%)
    pallas_call x1, Pallas kernels, device_step(): pl.pallas_call(functools.partial(whole_kernel, n), out_shape=(row_t, row_...  1140 us

profile of v5, /device:TPU:23, one launch (start us, length us, event | category | flops | bytes accessed | tf_op | source)
XLA Modules:
  0.0 1152.8 jit_solution(199739002481569840)
XLA Ops:
  0.6 1140.6 %whole.1 = (bf16[32,512,128]{2,1,0:T(8,128)(2,1)}, bf16[32,512,128]{2,1,0:T(8,128)(2,1)}, bf16[32,512,128]{2,1,0:T(8,128)(2,1)}, bf16[32,128,512]{2,1,0:T(8,128)...) custom-call(bf16[32,512,128]{2,1,0:T(8,128)(2,1)} %z_hbm.1, s32[32,512]{1,0:T(8,128)} %m_ref.1, ...), custom_call_target="tpu_custom_call" | custom-call | tf_op jit(solution)/shard_map/whole/pallas_call | solution.py:648
  1141.2 0.7 convert_element_type.3
  1142.0 0.6 pad_maximum_fusion.3
  1142.5 0.8 slice_bitcast_fusion.3
  1143.3 1.0 slice_bitcast_fusion.1
  1144.4 0.7 pad_maximum_fusion.1
  1145.1 0.9 copy.21
  1146.0 0.0 copy-start
  1146.0 4.8 copy.24
  1150.8 0.0 copy-done
  1150.8 2.0 copy.25
  (8 shorter events, 0.1 us)
Async XLA Ops:
  1146.0 4.8 copy-start
